TPU v7x, 256 devices: a whole 4x4x8 slice. The times are simulated.
256 devices in a mesh: pop: 32 (over z, y_lo, core), tp: 8 (over y_hi, x).
Axes of the slice: x: 4, y: 4 (y_hi: 2, y_lo: 2; y = y_hi * 2 + y_lo), z: 8, core: 2. Of those that a mesh axis runs over, the one named last changes fastest.
Arguments:
- tokens: bfloat16 [32, 512, 1792], P('pop', None, 'tp'), may hold values from -6 to 6
- weight: bfloat16 [32, 1792, 7168], P('pop', 'tp'), may hold values from -0.125 to 0.125
- momentum: bfloat16 [32, 1792, 7168], P('pop', 'tp'), may hold values from -6 to 6
- cotangent: bfloat16 [32, 512, 7168], P('pop', None, 'tp'), may hold values from -0.5 to 0.5
- assignment: int32 [8, 2], replicated, may hold values from 0 to 31, as said below
- lr_index: int32 [32], replicated, may hold values from 0 to 7
- rates: float32 [8], replicated, may hold values from 0.01 to 0.1
Outputs:
- activation: bfloat16 [32, 512, 7168], P('pop', None, 'tp')
- new_weight: bfloat16 [32, 1792, 7168], P('pop', 'tp')
Inputs may be any that keep to these rules, and one draw needn't show every extreme that they name: `assignment`: column 0 names 8 distinct members; column 1 names exactly 2 distinct members, each in some row, none of them in column 0.
All inputs are finite; a program needn't handle non-finite values.
Results may differ from a plain program's by a relative error of at most 0.015.
Values may be sent and summed in bfloat16 or wider, within the bound.
No kernel may reach another device: no remote copies, remote signals or barrier semaphores. Data moves between devices by JAX's collectives and lax.ppermute only.
A program may use at most 192 MiB of HBM per device.

v0:
```python
import jax
import jax.numpy as jnp
from jax import lax
from jax.sharding import PartitionSpec as P


def side_by_side(arrays, axis, split_dim, concat_dim, along):
    both = jnp.concatenate(arrays, axis=along)
    filled, at, done = (
        lax.all_to_all(both, axis, split_axis=split_dim, concat_axis=concat_dim, tiled=True),
        0,
        [],
    )
    for a in arrays:
        done.append(lax.slice_in_dim(filled, at, at + a.shape[along], axis=along))
        at += a.shape[along]
    return tuple(done)


def gelu_tanh(value):
    return jax.nn.gelu(value, approximate=True)


def activate(hidden, cot_block):
    active, pullback = jax.vjp(gelu_tanh, hidden)
    grad_hidden = pullback(cot_block.astype(jnp.float32))[0].astype(jnp.bfloat16)
    return (active.astype(jnp.bfloat16), grad_hidden)


def local(tokens, weight, momentum, cotangent, assignment, lr_index, rates):
    members = lax.axis_size("pop")
    me = lax.axis_index("pop")
    member_ids = jnp.arange(members, dtype=jnp.int32)
    hit = assignment[:, 0][None, :] == member_ids[:, None]
    source_all = jnp.where(
        jnp.any(hit, axis=1),
        jnp.sum(jnp.where(hit, assignment[:, 1][None, :], 0), axis=1),
        member_ids,
    )
    my_index = jnp.sum(jnp.where(member_ids == me, lr_index, 0))
    rate_ids = jnp.arange(rates.shape[0], dtype=jnp.int32)
    my_rate = jnp.sum(jnp.where(rate_ids == my_index, rates, 0.0))
    flat_weight = weight.reshape(members, -1)
    flat_momentum = momentum.reshape(members, -1)
    held = side_by_side((flat_weight, flat_momentum), "pop", 0, 0, 1)
    picked = (held[0][source_all], held[1][source_all])
    returned = side_by_side((picked[0], picked[1]), "pop", 0, 0, 1)
    taken_weight = returned[0].reshape(weight.shape)[0]
    taken_momentum = returned[1].reshape(momentum.shape)[0]
    inputs = tokens[0]
    partial_value = jnp.dot(inputs, taken_weight, preferred_element_type=jnp.float32)
    hidden_share = lax.psum_scatter(
        partial_value.astype(jnp.bfloat16), "tp", scatter_dimension=1, tiled=True
    ).astype(jnp.float32)
    activation, grad_share = activate(hidden_share, cotangent[0])
    grad_hidden = lax.all_gather(grad_share, "tp", axis=1, tiled=True)
    grad_weight = lax.dot_general(
        inputs, grad_hidden, (((0,), (0,)), ((), ())), preferred_element_type=jnp.float32
    )
    new_momentum = 0.9 * taken_momentum.astype(jnp.float32) + grad_weight
    updated = (taken_weight.astype(jnp.float32) - my_rate * new_momentum).astype(jnp.bfloat16)
    return (activation[None], updated[None])


def solution(mesh):
    placed = (
        P("pop", None, "tp"),
        P("pop", "tp", None),
        P("pop", "tp", None),
        P("pop", None, "tp"),
        P(),
        P(),
        P(),
    )
    return jax.shard_map(
        local,
        mesh=mesh,
        in_specs=placed,
        out_specs=(P("pop", None, "tp"), P("pop", "tp", None)),
        check_vma=False,
    )
```

profile of v0, /device:TPU:6, one launch (start us, length us, event | category | flops | bytes accessed | tf_op | source)
XLA Modules:
  0.0 700.0 jit_solution(3552922835400282896)
XLA Ops:
  7.2 5.6 reshape.46
  12.8 6.7 reshape.45
  19.5 5.0 maximum_bitcast_fusion
  25.0 9.3 %reduce = bf16[32,100352]{1,0:T(8,128)(2,1)} reduce(bf16[32,1,100352]{2,0,1:T(8,128)(2,1)} %maximum_bitcast_fusion, bf16[]{:T(256)} %broadcast.61), dimensions={1}, to_apply=%copy.18.reduce_sub_computation | reduce | bytes 12845058 | tf_op jit(solution)/shard_map/all_to_all | solution.py:10
  34.4 8.9 %reshape.64 = bf16[32,2,50176]{2,1,0:T(2,128)(2,1)} reshape(bf16[32,100352]{1,0:T(8,128)(2,1)} %reduce) | data formatting | bytes 12845056
  43.2 10.1 %all-to-all-start = ((bf16[32,2,50176]{2,1,0:T(2,128)(2,1)}), bf16[32,2,50176]{2,1,0:T(2,128)(2,1)}, u32[]{:S(2)}, u32[]{:S(2)}) async-start(bf16[32,2,50176]{2,1,0:T(2,128)(2,1)} %reshape.64), calls=%async_computation | async-start | bytes 12845056 | tf_op jit(solution)/shard_map/all_to_all | solution.py:10
  53.6 144.2 %all-to-all-done = bf16[32,2,50176]{2,1,0:T(2,128)(2,1)} async-done(((bf16[32,2,50176]{2,1,0:T(2,128)(2,1)}), bf16[32,2,50176]{2,1,0:T(2,128)(2,1)}, u32[]{:S(2)}, u32[]{:S(2)}) %all-to-all-start) | async-done | bytes 6422560 | tf_op jit(solution)/shard_map/all_to_all | solution.py:10
  197.8 21.5 %reshape.65 = bf16[32,1,100352]{2,1,0:T(2,128)(2,1)} reshape(bf16[32,2,50176]{2,1,0:T(2,128)(2,1)} %all-to-all-done) | data formatting | bytes 12845056
  219.3 11.0 %copy.27 = bf16[32,1,100352]{2,0,1:T(8,128)(2,1)} copy(bf16[32,1,100352]{2,1,0:T(2,128)(2,1)} %reshape.65) | data formatting | bytes 12845056
  230.3 5.0 fusion.24
  235.3 9.4 %gather_fusion.1 = bf16[32,50176]{1,0:T(8,128)(2,1)} fusion(bf16[32,50176]{1,0:T(8,128)(2,1)} %get-tuple-element.11, s32[1024]{0:T(1024)S(1)} %pad_clamp_fusion), kind=kCustom, calls=%fused_computation.1 | custom fusion | bytes 6422656 | tf_op jit(solution)/shard_map/gather | solution.py:46
  249.0 6.0 maximum_bitcast_fusion.1
  255.0 9.5 %reduce.1 = bf16[32,100352]{1,0:T(8,128)(2,1)} reduce(bf16[32,1,100352]{2,0,1:T(8,128)(2,1)} %maximum_bitcast_fusion.1, bf16[]{:T(256)} %broadcast.61), dimensions={1}, to_apply=%copy.19.reduce_sub_computation | reduce | bytes 12845058 | tf_op jit(solution)/shard_map/all_to_all | solution.py:10
  264.5 8.9 %reshape.66 = bf16[32,2,50176]{2,1,0:T(2,128)(2,1)} reshape(bf16[32,100352]{1,0:T(8,128)(2,1)} %reduce.1) | data formatting | bytes 12845056
  273.4 149.3 %all_to_all.24 = bf16[32,2,50176]{2,1,0:T(2,128)(2,1)} all-to-all(bf16[32,2,50176]{2,1,0:T(2,128)(2,1)} %reshape.66), channel_id=1, replica_groups=mesh['pop'=32,'tp'=8] {'pop'}, dimensions={0} | all-to-all | bytes 12845056 | tf_op jit(solution)/shard_map/all_to_all | solution.py:10
  422.7 21.3 %reshape.67 = bf16[32,1,100352]{2,1,0:T(2,128)(2,1)} reshape(bf16[32,2,50176]{2,1,0:T(2,128)(2,1)} %all_to_all.24) | data formatting | bytes 12845056
  443.9 11.1 %copy.26 = bf16[32,1,100352]{2,0,1:T(8,128)(2,1)} copy(bf16[32,1,100352]{2,1,0:T(2,128)(2,1)} %reshape.67) | data formatting | bytes 12845056
  458.8 5.5 squeeze_reshape.4
  464.3 5.1 fusion
  472.0 105.6 %reduce-scatter.2.cloned.1.call-done = bf16[512,896]{0,1:T(8,128)(2,1)} async-done(((bf16[512,7168]{0,1:T(8,128)(2,1)}), bf16[512,896]{0,1:T(8,128)(2,1)}) %reduce-scatter.2.cloned.1.call-update) | async-done | bytes 917520 | tf_op jit(solution)/shard_map/reduce_scatter | solution.py:52
  583.8 5.0 convert_multiply_fusion
  588.7 6.3 mul.66
  597.4 85.7 %all-gather.2.cloned.1.call-done = bf16[512,7168]{0,1:T(8,128)(2,1)} async-done(((bf16[512,896]{0,1:T(8,128)(2,1)}), bf16[512,7168]{0,1:T(8,128)(2,1)}) %all-gather.2.cloned.1.call-update) | async-done | bytes 7340048 | tf_op jit(solution)/shard_map/all_gather | solution.py:56
  683.1 9.6 %fusion.5 = bf16[1,224,7168]{2,1,0:T(8,128)(2,1)} fusion(f32[224,7168]{1,0:T(8,128)} %mul.66, bf16[512,7168]{0,1:T(8,128)(2,1)} %all-gather.2.cloned.1.call-done, bf16[224,7168]{1,0:T(8,128)(2,1)S(1)} %squeeze_reshape.4, f32[]{:T(128)} %fusion.22, bf16[1,512,224]{1,2,0:T(8,128)(2,1)S(1)} %copy-done), kind=kOutput, calls=%fused_computation.9 | convolution fusion | flops 1652195328 | bytes 20414468 | tf_op jit(solution)/shard_map/dot_general | solution.py:57
  (25 shorter events, 19.8 us)
Async XLA Ops:
  7.2 457.2 %copy-start = (bf16[1,512,224]{1,2,0:T(8,128)(2,1)S(1)}, bf16[1,512,224]{1,2,0:T(8,128)(2,1)}, u32[]{:S(2)}) copy-start(bf16[1,512,224]{1,2,0:T(8,128)(2,1)} %param.7) | copy-start | bytes 688132
  43.2 10.2 %copy-start.1 = (s32[8,2]{0,1:T(2,128)S(1)}, s32[8,2]{0,1:T(2,128)}, u32[]{:S(2)}) copy-start(s32[8,2]{0,1:T(2,128)} %param.11) | copy-start | bytes 196
  43.2 154.6 %all-to-all-start = ((bf16[32,2,50176]{2,1,0:T(2,128)(2,1)}), bf16[32,2,50176]{2,1,0:T(2,128)(2,1)}, u32[]{:S(2)}, u32[]{:S(2)}) async-start(bf16[32,2,50176]{2,1,0:T(2,128)(2,1)} %reshape.64), calls=%async_computation | async-start | bytes 12845056 | tf_op jit(solution)/shard_map/all_to_all | solution.py:10
  53.3 524.3 %reduce-scatter.2.cloned.1.call-start = ((), (), s32[]{:S(2)}) async-start(), calls=%async_computation.3 | async-start | bytes 8257536 | tf_op jit(solution)/shard_map/reduce_scatter | solution.py:52
  469.5 112.3 %copy-start.2 = (s32[32]{0:T(128)S(1)}, s32[32]{0:T(128)}, u32[]{:S(2)}) copy-start(s32[32]{0:T(128)} %param.12) | copy-start | bytes 388
  469.5 112.9 %copy-start.3 = (f32[8]{0:T(128)S(1)}, f32[8]{0:T(128)}, u32[]{:S(2)}) copy-start(f32[8]{0:T(128)} %param.13) | copy-start | bytes 100
  469.5 213.6 %all-gather.2.cloned.1.call-start = ((), (), s32[]{:S(2)}) async-start(), calls=%async_computation.4 | async-start | bytes 8257536 | tf_op jit(solution)/shard_map/all_gather | solution.py:56
Sparse Core Ops, SparseCore 0:
  469.6 107.9 reduce-scatter.1
  581.9 101.1 all-gather.1
where the time goes:
time: 710 us; the launch traced here: 700 us
  waiting for transfers between devices  336 us (47%)
  blocking collectives  149 us (21%)
  local copies, waits for them, and re-layouts  134 us (19%)
  other arithmetic  41.1 us (6%)
  matrix products  14.7 us (2%)
  between operations  14.6 us (2%)
  starting transfers between devices  10.2 us (1%)
    all_to_all x1, blocking collectives, side_by_side(): lax.all_to_all(both, axis, split_axis=split_dim, concat_axis=concat_dim,...  149 us
    all_to_all x1, waiting for transfers between devices, side_by_side(): lax.all_to_all(both, axis, split_axis=split_dim, concat_axis=concat_dim,...  144 us
    reduce_scatter x1, waiting for transfers between devices, local(): lax.psum_scatter(partial_value.astype(jnp.bfloat16), 'tp', scatter_dimens...  106 us
    unnamed x16, local copies, waits for them, and re-layouts  87.4 us
    all_gather x1, waiting for transfers between devices, local(): grad_hidden = lax.all_gather(grad_share, 'tp', axis=1, tiled=True)  85.7 us
    all_to_all x4, other arithmetic, side_by_side(): lax.all_to_all(both, axis, split_axis=split_dim, concat_axis=concat_dim,...  29.9 us
  transfers between devices with their start and end apart: 3, of which 3 were waited for; matrix products, arithmetic and copies ran while one was open for 3% of the time, Pallas kernels for 0%

commit v1 on v0

v1 whole, which is shorter than its diff:
```python
import jax
import jax.numpy as jnp
from jax import lax
from jax.experimental import pallas as pl
from jax.experimental.pallas import tpu as pltpu
from jax.sharding import Mesh, PartitionSpec as P

POP = ("z", "yl", "c")
TP = ("yh", "x")
NZ = 8
NK = 8
GELU_A = 0.7978845608028654
GELU_B = 0.044715

MINE_A, MINE_B, THEIRS_A, THEIRS_B, CORE, LOSER, SLOT = range(7)


def params(n=1):
    return pltpu.CompilerParams(
        dimension_semantics=("arbitrary",) * n, vmem_limit_bytes=48 * 1024 * 1024
    )


def slots_kernel(tab, mine, theirs, out):
    zero = jnp.zeros(mine.shape, mine.dtype)
    m, t = mine[...], theirs[...]
    for s, (own, other) in enumerate(((MINE_A, THEIRS_A), (MINE_B, THEIRS_B))):
        out[0, s] = jnp.where(tab[own] == 1, m, jnp.where(tab[other] == 1, t, zero))


def build_slots(tab, shard, theirs):
    half, width = shard.shape[0] // 2, shard.shape[1] // NZ
    return pl.pallas_call(
        slots_kernel,
        grid_spec=pltpu.PrefetchScalarGridSpec(
            num_scalar_prefetch=1,
            grid=(NZ,),
            in_specs=[
                pl.BlockSpec((half, width), lambda j, tab: (tab[CORE], j)),
                pl.BlockSpec((half, width), lambda j, tab: (0, j)),
            ],
            out_specs=pl.BlockSpec((1, 2, half, width), lambda j, tab: (j, 0, 0, 0)),
        ),
        out_shape=jax.ShapeDtypeStruct((NZ, 2, half, width), shard.dtype),
        compiler_params=params(),
        cost_estimate=pl.CostEstimate(flops=5_000_000, bytes_accessed=10_000_000, transcendentals=0),
        name="slots",
    )(tab, shard, theirs)


def joined(tab, gathered, received):
    g, r = gathered[0, 0], received[0]
    first = tab[CORE] == 0
    return jnp.where(first, g, r), jnp.where(first, r, g)


def take_kernel(tab, own, gathered, received, out):
    half = received.shape[1]
    low, high = joined(tab, gathered, received)
    loser = tab[LOSER] == 1
    out[0, :half] = jnp.where(loser, low, own[:half])
    out[0, half:] = jnp.where(loser, high, own[half:])


def taken_specs(rows, half, width):
    return [
        pl.BlockSpec((rows, width), lambda j, tab, *_: (0, j)),
        pl.BlockSpec((1, 1, half, width), lambda j, tab, *_: (j, tab[SLOT], 0, 0)),
        pl.BlockSpec((1, half, width), lambda j, tab, *_: (j, 0, 0)),
    ]


def take(tab, shard, gathered, received):
    rows, width = shard.shape[0], shard.shape[1] // NZ
    return pl.pallas_call(
        take_kernel,
        grid_spec=pltpu.PrefetchScalarGridSpec(
            num_scalar_prefetch=1,
            grid=(NZ,),
            in_specs=taken_specs(rows, rows // 2, width),
            out_specs=pl.BlockSpec((1, rows, width), lambda j, tab: (j, 0, 0)),
        ),
        out_shape=jax.ShapeDtypeStruct((NZ, rows, width), shard.dtype),
        compiler_params=params(),
        cost_estimate=pl.CostEstimate(flops=5_000_000, bytes_accessed=10_000_000, transcendentals=0),
        name="take",
    )(tab, shard, gathered, received)


def final_kernel(tab, rate, own, gathered, received, back, out):
    half = received.shape[1]
    low, high = joined(tab, gathered, received)
    loser = tab[LOSER] == 1
    scale = 0.9 * rate[0]
    for at, piece in ((0, low), (half, high)):
        rows = pl.ds(at, half)
        m = jnp.where(loser, piece, own[rows]).astype(jnp.float32)
        out[rows] = (back[0, rows].astype(jnp.float32) - scale * m).astype(out.dtype)


def final(tab, rate, shard, gathered, received, back):
    rows, width = shard.shape[0], shard.shape[1] // NZ
    return pl.pallas_call(
        final_kernel,
        grid_spec=pltpu.PrefetchScalarGridSpec(
            num_scalar_prefetch=2,
            grid=(NZ,),
            in_specs=taken_specs(rows, rows // 2, width)
            + [pl.BlockSpec((1, rows, width), lambda j, tab, rate: (j, 0, 0))],
            out_specs=pl.BlockSpec((rows, width), lambda j, tab, rate: (0, j)),
        ),
        out_shape=jax.ShapeDtypeStruct(shard.shape, shard.dtype),
        compiler_params=params(),
        cost_estimate=pl.CostEstimate(flops=5_000_000, bytes_accessed=13_000_000, transcendentals=0),
        name="final",
    )(tab, rate, shard, gathered, received, back)


def step_kernel(rate, tokens, weight, cot, act, back, acc, grad):
    i = pl.program_id(0)

    @pl.when(i == 0)
    def _():
        acc[...] = jnp.zeros_like(acc)

    @pl.when(i < NK)
    def _():
        acc[...] += lax.dot_general(
            tokens[0], weight[0], (((0,), (0,)), ((), ())), preferred_element_type=jnp.float32
        )

    @pl.when(i == NK - 1)
    def _():
        v = acc[...]
        t = jnp.tanh(GELU_A * (v + GELU_B * (v * v * v)))
        act[...] = (0.5 * v * (1.0 + t)).astype(act.dtype)
        slope = 0.5 * (1.0 + t) + 0.5 * v * (1.0 - t * t) * (GELU_A * (1.0 + 3.0 * GELU_B * (v * v)))
        grad[...] = (cot[...].astype(jnp.float32) * slope).astype(grad.dtype)

    @pl.when(i >= NK)
    def _():
        gw = jnp.dot(tokens[0], grad[...], preferred_element_type=jnp.float32)
        back[0] = (weight[0].astype(jnp.float32) - rate[0] * gw).astype(back.dtype)


def step(rate, tokens, weight, cot):
    nk, r, t = tokens.shape
    f = weight.shape[2]
    return pl.pallas_call(
        step_kernel,
        grid_spec=pltpu.PrefetchScalarGridSpec(
            num_scalar_prefetch=1,
            grid=(2 * NK,),
            in_specs=[
                pl.BlockSpec((1, r, t), lambda i, rate: (lax.rem(i, NK), 0, 0)),
                pl.BlockSpec((1, r, f), lambda i, rate: (lax.rem(i, NK), 0, 0)),
                pl.BlockSpec((t, f), lambda i, rate: (0, 0)),
            ],
            out_specs=[
                pl.BlockSpec((t, f), lambda i, rate: (0, 0)),
                pl.BlockSpec((1, r, f), lambda i, rate: (jnp.maximum(i - NK, 0), 0, 0)),
            ],
            scratch_shapes=[pltpu.VMEM((t, f), jnp.float32), pltpu.VMEM((t, f), jnp.bfloat16)],
        ),
        out_shape=[
            jax.ShapeDtypeStruct((t, f), jnp.bfloat16),
            jax.ShapeDtypeStruct((nk, r, f), jnp.bfloat16),
        ],
        compiler_params=params(),
        cost_estimate=pl.CostEstimate(
            flops=4 * nk * t * r * f, bytes_accessed=20_000_000, transcendentals=t * f
        ),
        name="step",
    )(rate, tokens, weight, cot)


def swap_core(x):
    return lax.ppermute(x, "c", [(0, 1), (1, 0)])


def own_slots(tab, shard, core):
    half = shard.shape[0] // 2
    theirs = swap_core(lax.dynamic_slice_in_dim(shard, (1 - core) * half, half, axis=0))
    return build_slots(tab, shard, theirs)


def scatter(slots):
    return lax.psum_scatter(slots, "z", scatter_dimension=0, tiled=True)


def gather(mine):
    mine = mine + lax.ppermute(mine, "yl", [(0, 1), (1, 0)])
    return lax.all_gather(mine, "z", axis=0, tiled=True)


def other_half(gathered, slot):
    return swap_core(lax.dynamic_index_in_dim(gathered, slot, axis=1, keepdims=False))


def local(tokens, weight, momentum, cotangent, assignment, lr_index, rates):
    core = lax.axis_index("c")
    me = lax.axis_index(POP)
    partner = me + 1 - 2 * core
    loser_ids, winner_ids = assignment[:, 0], assignment[:, 1]
    win_a, win_b = jnp.min(winner_ids), jnp.max(winner_ids)

    def slot_of(member):
        hit = loser_ids == member
        return jnp.any(hit), jnp.any(hit & (winner_ids == win_b)).astype(jnp.int32)

    loser, slot = slot_of(me)
    _, partner_slot = slot_of(partner)
    tab = jnp.stack(
        [
            (win_a == me).astype(jnp.int32),
            (win_b == me).astype(jnp.int32),
            (win_a == partner).astype(jnp.int32),
            (win_b == partner).astype(jnp.int32),
            core.astype(jnp.int32),
            loser.astype(jnp.int32),
            slot,
        ]
    )
    member_ids = jnp.arange(lr_index.shape[0], dtype=jnp.int32)
    my_index = jnp.sum(jnp.where(member_ids == me, lr_index, 0))
    rate_ids = jnp.arange(rates.shape[0], dtype=jnp.int32)
    rate = jnp.sum(jnp.where(rate_ids == my_index, rates, 0.0)).reshape(1)

    w, m = weight[0], momentum[0]
    w_slots, m_slots = own_slots(tab, w, core), own_slots(tab, m, core)
    turned = jnp.swapaxes(tokens, 1, 2)
    all_tokens = lax.all_to_all(
        jnp.broadcast_to(turned, (NK,) + turned.shape[1:]), TP, 0, 0, tiled=True
    )
    w_mine, all_tokens = lax.optimization_barrier((scatter(w_slots), all_tokens))
    w_won = gather(w_mine)
    m_slots, w_won = lax.optimization_barrier((m_slots, w_won))
    m_mine = scatter(m_slots)
    w_taken = take(tab, w, w_won, other_half(w_won, partner_slot))
    w_columns = lax.all_to_all(w_taken, TP, 0, 0, tiled=True)
    m_mine, w_columns = lax.optimization_barrier((m_mine, w_columns))
    m_won = gather(m_mine)
    activation, back = step(rate, all_tokens, w_columns, cotangent[0])
    back = lax.all_to_all(back, TP, 0, 0, tiled=True)
    updated = final(tab, rate, m, m_won, other_half(m_won, partner_slot), back)
    return (activation[None], updated[None])


def solution(mesh):
    fine = Mesh(mesh.devices.reshape(8, 2, 2, 2, 4), POP + TP)
    placed = (
        P(POP, None, TP),
        P(POP, TP, None),
        P(POP, TP, None),
        P(POP, None, TP),
        P(),
        P(),
        P(),
    )
    return jax.shard_map(
        local,
        mesh=fine,
        in_specs=placed,
        out_specs=(P(POP, None, TP), P(POP, TP, None)),
        check_vma=False,
    )
```

time: 710 us -> 279 us (0.39); the launches traced: 700 us -> 278 us
  waiting for transfers between devices: 336 us -> 115 us
  local copies, waits for them, and re-layouts: 134 us -> 6.72 us
  blocking collectives: 149 us -> 78 us
  Pallas kernels: 0 us -> 42.8 us
  other arithmetic: 41.1 us -> 7.61 us
  matrix products: 14.7 us -> 0 us
    all_to_all x1, waiting for transfers between devices: 144 us -> 21.5 us  [local(): back = lax.all_to_all(back, TP, 0, 0, tiled=True)]
    reduce_scatter x1 -> x2, waiting for transfers between devices: 106 us -> 17.7 us  [scatter(): return lax.psum_scatter(slots, 'z', scatter_dimension=0, tiled=True)]
    unnamed x16 -> x18, local copies, waits for them, and re-layouts: 87.4 us -> 1.92 us
    all_to_all x1 -> x2, blocking collectives: 149 us -> 78 us  [the longest x1 46.2 us: local(): w_columns = lax.all_to_all(w_taken, TP, 0, 0, tiled=True)]
    pallas_call x0 -> x5, Pallas kernels: none -> 42.8 us  [the longest x1 16 us: step(): pl.pallas_call(step_kernel, grid_spec=pltpu.PrefetchScalarGridSpec(num_sc...]
    all_gather x1 -> x2, waiting for transfers between devices: 85.7 us -> 51.9 us  [gather(): return lax.all_gather(mine, 'z', axis=0, tiled=True)]
    all_to_all x4 -> x0, other arithmetic: 29.9 us -> none  [side_by_side(): lax.all_to_all(both, axis, split_axis=split_dim, concat_axis=concat_dim,...]
    ppermute x0 -> x6, waiting for transfers between devices: none -> 23.5 us  [the longest x2 16.6 us: gather(): mine = mine + lax.ppermute(mine, 'yl', [(0, 1), (1, 0)])]
  transfers between devices with their start and end apart: 3 -> 11, of which waited for: 3 -> 8; matrix products, arithmetic and copies ran while one was open for 3% -> 3% of each run, Pallas kernels for 0% -> 10%
where the time goes in v1:
time: 279 us; the launch traced here: 278 us
  waiting for transfers between devices  115 us (41%)
  blocking collectives  78 us (28%)
  Pallas kernels  42.8 us (15%)
  between operations  18.4 us (7%)
  starting transfers between devices  9.63 us (3%)
  other arithmetic  7.61 us (3%)
  local copies, waits for them, and re-layouts  6.72 us (2%)
    all_gather x2, waiting for transfers between devices, gather(): return lax.all_gather(mine, 'z', axis=0, tiled=True)  51.9 us
    all_to_all x1, blocking collectives, local(): w_columns = lax.all_to_all(w_taken, TP, 0, 0, tiled=True)  46.2 us
    all_to_all x1, blocking collectives, local(): lax.all_to_all(jnp.broadcast_to(turned, (NK,) + turned.shape[1:]), TP, 0,...  31.7 us
    all_to_all x1, waiting for transfers between devices, local(): back = lax.all_to_all(back, TP, 0, 0, tiled=True)  21.5 us
    reduce_scatter x2, waiting for transfers between devices, scatter(): return lax.psum_scatter(slots, 'z', scatter_dimension=0, tiled=True)  17.7 us
    ppermute x2, waiting for transfers between devices, gather(): mine = mine + lax.ppermute(mine, 'yl', [(0, 1), (1, 0)])  16.6 us
    pallas_call x1, Pallas kernels, step(): pl.pallas_call(step_kernel, grid_spec=pltpu.PrefetchScalarGridSpec(num_sc...  16 us
    pallas_call x2, Pallas kernels, build_slots(): pl.pallas_call(slots_kernel, grid_spec=pltpu.PrefetchScalarGridSpec(num_s...  12.9 us
  transfers between devices with their start and end apart: 11, of which 8 were waited for; matrix products, arithmetic and copies ran while one was open for 3% of the time, Pallas kernels for 10%

profile of v1, /device:TPU:6, one launch (start us, length us, event | category | flops | bytes accessed | tf_op | source)
XLA Modules:
  0.0 277.7 jit_solution(7905345136286012851)
XLA Ops:
  7.2 1.5 dynamic-slice_bitcast_fusion.3
  11.9 1.4 and_reduce_fusion
  14.7 6.5 %slots.2 = bf16[8,2,112,896]{3,2,1,0:T(8,128)(2,1)} custom-call(s32[7]{0:T(128)S(1)} %stack.55.tab, bf16[224,7168]{1,0:T(8,128)(2,1)} %bitcast.27, bf16[112,7168]{1,0:T(8,128)(2,1)S(1)} %collective-permute-done.theirs), custom_call_target="tpu_custom_call" | custom-call | flops 5000000 | bytes 10000000 | tf_op jit(solution)/shard_map/slots/pallas_call | solution.py:33
  22.2 31.7 %all_to_all.15.tokens = bf16[8,224,512]{2,1,0:T(8,128)(2,1)} all-to-all(bf16[8,224,512]{2,1,0:T(8,128)(2,1)S(1)} %broadcast_in_dim.24), channel_id=1, replica_groups=mesh['z'=8,'yl'=2,'c'=2,'yh'=2,'x'=4] {'yh','x'}, dimensions={0} | all-to-all | bytes 3670016 | tf_op jit(solution)/shard_map/all_to_all | solution.py:232
  53.9 17.7 %reduce-scatter.3.cloned.1.call-done = bf16[1,2,112,896]{3,2,1,0:T(8,128)(2,1)} async-done(((bf16[8,2,112,896]{3,2,1,0:T(8,128)(2,1)}), bf16[1,2,112,896]{3,2,1,0:T(8,128)(2,1)}) %reduce-scatter.3.cloned.1.call-update) | async-done | bytes 401424 | tf_op jit(solution)/shard_map/reduce_scatter | solution.py:188
  71.6 1.6 collective-permute-start.2
  73.2 7.1 %collective-permute-done.2 = bf16[1,2,112,896]{3,2,1,0:T(8,128)(2,1)S(1)} collective-permute-done((bf16[1,2,112,896]{3,2,1,0:T(8,128)(2,1)}, bf16[1,2,112,896]{3,2,1,0:T(8,128)(2,1)S(1)}, u32[]{:S(2)}, u32[]{:S(2)}) %collective-permute-start.2) | collective-permute-done | bytes 401440 | tf_op jit(solution)/shard_map/ppermute | solution.py:192
  80.3 1.9 add.32
  82.5 3.4 %collective-permute-done.1.theirs = bf16[112,7168]{1,0:T(8,128)(2,1)S(1)} collective-permute-done((bf16[112,7168]{1,0:T(8,128)(2,1)S(1)}, bf16[112,7168]{1,0:T(8,128)(2,1)S(1)}, u32[]{:S(2)}, u32[]{:S(2)}) %collective-permute-start.1) | collective-permute-done | bytes 1605664 | tf_op jit(solution)/shard_map/ppermute | solution.py:178
  85.9 6.5 %slots.3 = bf16[8,2,112,896]{3,2,1,0:T(8,128)(2,1)} custom-call(s32[7]{0:T(128)S(1)} %stack.55.tab, bf16[224,7168]{1,0:T(8,128)(2,1)} %bitcast.24, bf16[112,7168]{1,0:T(8,128)(2,1)S(1)} %collective-permute-done.1.theirs), custom_call_target="tpu_custom_call" | custom-call | flops 5000000 | bytes 10000000 | tf_op jit(solution)/shard_map/slots/pallas_call | solution.py:33
  92.4 34.8 %all-gather.3.cloned.1.call-done.gathered = bf16[8,2,112,896]{3,2,1,0:T(8,128)(2,1)} async-done(((bf16[1,2,112,896]{3,2,1,0:T(8,128)(2,1)}), bf16[8,2,112,896]{3,2,1,0:T(8,128)(2,1)}) %all-gather.3.cloned.1.call-update) | async-done | bytes 3211280 | tf_op jit(solution)/shard_map/all_gather | solution.py:193
  128.1 1.0 copy-done.4
  129.3 3.4 %collective-permute-done.3.received = bf16[8,112,896]{2,1,0:T(8,128)(2,1)S(1)} collective-permute-done((bf16[8,112,896]{2,1,0:T(8,128)(2,1)S(1)}, bf16[8,112,896]{2,1,0:T(8,128)(2,1)S(1)}, u32[]{:S(2)}, u32[]{:S(2)}) %collective-permute-start.3) | collective-permute-done | bytes 1605664 | tf_op jit(solution)/shard_map/ppermute | solution.py:178
  132.8 5.4 %take.1 = bf16[8,224,896]{2,1,0:T(8,128)(2,1)S(1)} custom-call(s32[7]{0:T(128)S(1)} %stack.55.tab, bf16[224,7168]{1,0:T(8,128)(2,1)} %bitcast.28, bf16[8,2,112,896]{3,2,1,0:T(8,128)(2,1)} %all-gather.3.cloned.1.call-done.gathered, bf16[8,112,896]{2,1,0:T(8,128)(2,1)S(1)} %collective-permute-done.3.received), custom_call_target="tpu_custom_call" | custom-call | flops 5000000 | bytes 10000000 | tf_op jit(solution)/shard_map/take/pallas_call | solution.py:75
  138.3 46.2 %all_to_all.16.weight = bf16[8,224,896]{2,1,0:T(8,128)(2,1)} all-to-all(bf16[8,224,896]{2,1,0:T(8,128)(2,1)S(1)} %take.1), channel_id=1, replica_groups=mesh['z'=8,'yl'=2,'c'=2,'yh'=2,'x'=4] {'yh','x'}, dimensions={0} | all-to-all | bytes 6422528 | tf_op jit(solution)/shard_map/all_to_all | solution.py:240
  185.1 9.5 %collective-permute-done.4 = bf16[1,2,112,896]{3,2,1,0:T(8,128)(2,1)S(1)} collective-permute-done((bf16[1,2,112,896]{3,2,1,0:T(8,128)(2,1)}, bf16[1,2,112,896]{3,2,1,0:T(8,128)(2,1)S(1)}, u32[]{:S(2)}, u32[]{:S(2)}) %collective-permute-start.4) | collective-permute-done | bytes 401440 | tf_op jit(solution)/shard_map/ppermute | solution.py:192
  194.6 1.9 add.34
  197.2 1.2 fusion.1
  198.4 16.0 %step.1 = (bf16[512,896]{1,0:T(8,128)(2,1)}, bf16[8,224,896]{2,1,0:T(8,128)(2,1)}) custom-call(f32[1]{0:T(128)} %bitcast.rate, bf16[8,224,512]{2,1,0:T(8,128)(2,1)S(1)} %copy-done.2, bf16[8,224,896]{2,1,0:T(8,128)(2,1)} %all_to_all.16.weight, bf16[512,896]{1,0:T(8,128)(2,1)S(1)} %bitcast.26), custom_call_target="tpu_custom_call" | custom-call | flops 3288334336 | bytes 20000000 | tf_op jit(solution)/shard_map/step/pallas_call | solution.py:149
  214.4 7.1 %all-to-all-start.2 = ((bf16[8,224,896]{2,1,0:T(8,128)(2,1)}), bf16[8,224,896]{2,1,0:T(8,128)(2,1)}, u32[]{:S(2)}, u32[]{:S(2)}) async-start(bf16[8,224,896]{2,1,0:T(8,128)(2,1)} %get-tuple-element.17), calls=%async_computation.4 | async-start | bytes 6422528 | tf_op jit(solution)/shard_map/all_to_all | solution.py:244
  221.4 17.0 %all-gather.5.cloned.1.call-done.gathered = bf16[8,2,112,896]{3,2,1,0:T(8,128)(2,1)} async-done(((bf16[1,2,112,896]{3,2,1,0:T(8,128)(2,1)}), bf16[8,2,112,896]{3,2,1,0:T(8,128)(2,1)}) %all-gather.5.cloned.1.call-update) | async-done | bytes 3211280 | tf_op jit(solution)/shard_map/all_gather | solution.py:193
  238.5 2.8 %dynamic-slice_bitcast_fusion = bf16[8,112,896]{2,1,0:T(8,128)(2,1)} fusion(bf16[8,2,112,896]{3,2,1,0:T(8,128)(2,1)} %all-gather.5.cloned.1.call-done.gathered, s32[]{:T(128)S(6)} %select_n.20), kind=kLoop, calls=%fused_computation | loop fusion | bytes 3211268 | tf_op jit(solution)/shard_map/jit(dynamic_index_in_dim)/squeeze | solution.py:197
  241.3 21.5 %all-to-all-done.2.back = bf16[8,224,896]{2,1,0:T(8,128)(2,1)} async-done(((bf16[8,224,896]{2,1,0:T(8,128)(2,1)}), bf16[8,224,896]{2,1,0:T(8,128)(2,1)}, u32[]{:S(2)}, u32[]{:S(2)}) %all-to-all-start.2) | async-done | bytes 3211296 | tf_op jit(solution)/shard_map/all_to_all | solution.py:244
  262.7 8.4 %final.1 = bf16[224,7168]{1,0:T(8,128)(2,1)} custom-call(s32[7]{0:T(128)S(1)} %stack.55.tab, f32[1]{0:T(128)} %bitcast.rate, bf16[224,7168]{1,0:T(8,128)(2,1)S(1)} %bitcast.25, bf16[8,2,112,896]{3,2,1,0:T(8,128)(2,1)} %all-gather.5.cloned.1.call-done.gathered, bf16[8,112,896]{2,1,0:T(8,128)(2,1)} %collective-permute-done.5.received, ...), custom_call_target="tpu_custom_call" | custom-call | flops 5000000 | bytes 13000000 | tf_op jit(solution)/shard_map/final/pallas_call | solution.py:103
  (39 shorter events, 3.7 us)
Async XLA Ops:
  7.2 1.7 copy-start.6
  7.2 64.5 %reduce-scatter.3.cloned.1.call-start = ((), (), s32[]{:S(2)}) async-start(), calls=%async_computation.5 | async-start | bytes 3612672 | tf_op jit(solution)/shard_map/reduce_scatter | solution.py:188
  8.8 5.9 %collective-permute-start = (bf16[112,7168]{1,0:T(8,128)(2,1)S(1)}, bf16[112,7168]{1,0:T(8,128)(2,1)S(1)}, u32[]{:S(2)}, u32[]{:S(2)}) collective-permute-start(bf16[112,7168]{1,0:T(8,128)(2,1)S(1)} %dynamic-slice_bitcast_fusion.3), channel_id=1, source_target_pairs={{0,8},{8,0},{1,9},{9,1},{2,10},{10,2},{3,11},{11,3},{4,12},{12,4},... | collective-permute-start | bytes 4816904 | tf_op jit(solution)/shard_map/ppermute | solution.py:178
  21.1 0.9 copy-start.5
  21.2 106.0 %all-gather.3.cloned.1.call-start = ((), (), s32[]{:S(2)}) async-start(), calls=%async_computation.6 | async-start | bytes 3612672 | tf_op jit(solution)/shard_map/all_gather | solution.py:193
  22.1 60.2 %copy-start = (bf16[1,224,7168]{2,1,0:T(8,128)(2,1)S(1)}, bf16[1,224,7168]{2,1,0:T(8,128)(2,1)}, u32[]{:S(2)}) copy-start(bf16[1,224,7168]{2,1,0:T(8,128)(2,1)} %param.9) | copy-start | bytes 9633796
  71.6 8.7 %collective-permute-start.2 = (bf16[1,2,112,896]{3,2,1,0:T(8,128)(2,1)}, bf16[1,2,112,896]{3,2,1,0:T(8,128)(2,1)S(1)}, u32[]{:S(2)}, u32[]{:S(2)}) collective-permute-start(bf16[1,2,112,896]{3,2,1,0:T(8,128)(2,1)} %reduce-scatter.3.cloned.1.call-done), channel_id=1, source_target_pairs={{0,16},{16,0},{1,17},{17,1},{2,18},{18,2},{3,19},{19,3},{4,20},{20... | collective-permute-start | bytes 1204232 | tf_op jit(solution)/shard_map/ppermute | solution.py:192
  82.2 102.3 %reduce-scatter.5.cloned.1.call-start = ((), (), s32[]{:S(2)}) async-start(), calls=%async_computation.7 | async-start | bytes 3612672 | tf_op jit(solution)/shard_map/reduce_scatter | solution.py:188
  82.4 3.5 %collective-permute-start.1 = (bf16[112,7168]{1,0:T(8,128)(2,1)S(1)}, bf16[112,7168]{1,0:T(8,128)(2,1)S(1)}, u32[]{:S(2)}, u32[]{:S(2)}) collective-permute-start(bf16[112,7168]{1,0:T(8,128)(2,1)S(1)} %dynamic-slice_bitcast_fusion.2), channel_id=1, source_target_pairs={{0,8},{8,0},{1,9},{9,1},{2,10},{10,2},{3,11},{11,3},{4,12},{12,4},... | collective-permute-start | bytes 4816904 | tf_op jit(solution)/shard_map/ppermute | solution.py:178
  127.2 1.9 copy-start.4
  127.2 111.2 %all-gather.5.cloned.1.call-start = ((), (), s32[]{:S(2)}) async-start(), calls=%async_computation.8 | async-start | bytes 3612672 | tf_op jit(solution)/shard_map/all_gather | solution.py:193
  129.2 3.5 %collective-permute-start.3 = (bf16[8,112,896]{2,1,0:T(8,128)(2,1)S(1)}, bf16[8,112,896]{2,1,0:T(8,128)(2,1)S(1)}, u32[]{:S(2)}, u32[]{:S(2)}) collective-permute-start(bf16[8,112,896]{2,1,0:T(8,128)(2,1)S(1)} %dynamic-slice_bitcast_fusion.1), channel_id=1, source_target_pairs={{0,8},{8,0},{1,9},{9,1},{2,10},{10,2},{3,11},{11,3},{4,12},{12,4},... | collective-permute-start | bytes 4816904 | tf_op jit(solution)/shard_map/ppermute | solution.py:178
  138.2 58.3 %copy-start.7 = (s32[32]{0:T(128)S(1)}, s32[32]{0:T(128)}, u32[]{:S(2)}) copy-start(s32[32]{0:T(128)} %param.12) | copy-start | bytes 388
  138.2 58.9 %copy-start.8 = (f32[8]{0:T(128)S(1)}, f32[8]{0:T(128)}, u32[]{:S(2)}) copy-start(f32[8]{0:T(128)} %param.13) | copy-start | bytes 100
  138.2 60.1 %copy-start.2 = (bf16[8,224,512]{2,1,0:T(8,128)(2,1)S(1)}, bf16[8,224,512]{2,1,0:T(8,128)(2,1)}, u32[]{:S(2)}) copy-start(bf16[8,224,512]{2,1,0:T(8,128)(2,1)} %all_to_all.15.tokens) | copy-start | bytes 5505028
  138.3 60.1 %copy-start.3 = (bf16[1,512,896]{2,1,0:T(8,128)(2,1)S(1)}, bf16[1,512,896]{2,1,0:T(8,128)(2,1)}, u32[]{:S(2)}) copy-start(bf16[1,512,896]{2,1,0:T(8,128)(2,1)} %param.10) | copy-start | bytes 2752516
  184.5 10.1 %collective-permute-start.4 = (bf16[1,2,112,896]{3,2,1,0:T(8,128)(2,1)}, bf16[1,2,112,896]{3,2,1,0:T(8,128)(2,1)S(1)}, u32[]{:S(2)}, u32[]{:S(2)}) collective-permute-start(bf16[1,2,112,896]{3,2,1,0:T(8,128)(2,1)} %reduce-scatter.5.cloned.1.call-done), channel_id=1, source_target_pairs={{0,16},{16,0},{1,17},{17,1},{2,18},{18,2},{3,19},{19,3},{4,20},{20... | collective-permute-start | bytes 1204232 | tf_op jit(solution)/shard_map/ppermute | solution.py:192
  214.4 48.4 %all-to-all-start.2 = ((bf16[8,224,896]{2,1,0:T(8,128)(2,1)}), bf16[8,224,896]{2,1,0:T(8,128)(2,1)}, u32[]{:S(2)}, u32[]{:S(2)}) async-start(bf16[8,224,896]{2,1,0:T(8,128)(2,1)} %get-tuple-element.17), calls=%async_computation.4 | async-start | bytes 6422528 | tf_op jit(solution)/shard_map/all_to_all | solution.py:244
  221.4 41.3 %copy-start.1 = (bf16[1,224,7168]{2,1,0:T(8,128)(2,1)S(1)}, bf16[1,224,7168]{2,1,0:T(8,128)(2,1)}, u32[]{:S(2)}) copy-start(bf16[1,224,7168]{2,1,0:T(8,128)(2,1)} %param.9) | copy-start | bytes 9633796
  241.3 21.5 %collective-permute-start.5 = (bf16[8,112,896]{2,1,0:T(8,128)(2,1)}, bf16[8,112,896]{2,1,0:T(8,128)(2,1)}, u32[]{:S(2)}, u32[]{:S(2)}) collective-permute-start(bf16[8,112,896]{2,1,0:T(8,128)(2,1)} %dynamic-slice_bitcast_fusion), channel_id=1, source_target_pairs={{0,8},{8,0},{1,9},{9,1},{2,10},{10,2},{3,11},{11,3},{4,12},{12,4},... | collective-permute-start | bytes 4816904 | tf_op jit(solution)/shard_map/ppermute | solution.py:178
Sparse Core Ops, SparseCore 0:
  21.3 50.3 reduce-scatter.2
  82.3 44.8 all-gather.2
  130.3 45.8 reduce-scatter.4
  196.6 41.7 all-gather.4

commit v2 on v1

v2 whole, which is shorter than its diff:
```python
import jax
import jax.numpy as jnp
from jax import lax
from jax.experimental import pallas as pl
from jax.experimental.pallas import tpu as pltpu
from jax.sharding import Mesh, PartitionSpec as P

POP = ("z", "yl", "c")
TP = ("yh", "x")
NZ = 8
NK = 8
ROWS = 16
PAIR = 2
GELU_A = 0.7978845608028654
GELU_B = 0.044715

MINE_A, MINE_B, THEIRS_A, THEIRS_B, CORE, LOSER, SLOT, PLANE = range(8)
DISTANCES = (0, -1, 1, -2, 2, -3, 3, 4)


def params(n=1):
    return pltpu.CompilerParams(
        dimension_semantics=("arbitrary",) * n, vmem_limit_bytes=48 * 1024 * 1024
    )


def slots_kernel(tab, mine, theirs, out):
    pair, _, half, width = out.shape
    zero = jnp.zeros((half, width), mine.dtype)
    for j in range(pair):
        at = slice(j * width, (j + 1) * width)
        for s, (own, other) in enumerate(((MINE_A, THEIRS_A), (MINE_B, THEIRS_B))):
            out[j, s] = jnp.where(
                tab[own] == 1, mine[:, at], jnp.where(tab[other] == 1, theirs[:, at], zero)
            )


def build_slots(tab, shard, theirs):
    half, width = shard.shape[0] // 2, shard.shape[1] // NZ
    return pl.pallas_call(
        slots_kernel,
        grid_spec=pltpu.PrefetchScalarGridSpec(
            num_scalar_prefetch=1,
            grid=(NZ // PAIR,),
            in_specs=[
                pl.BlockSpec((half, PAIR * width), lambda j, tab: (tab[CORE], j)),
                pl.BlockSpec((half, PAIR * width), lambda j, tab: (0, j)),
            ],
            out_specs=pl.BlockSpec((PAIR, 2, half, width), lambda j, tab: (j, 0, 0, 0)),
        ),
        out_shape=jax.ShapeDtypeStruct((NZ, 2, half, width), shard.dtype),
        compiler_params=params(),
        cost_estimate=pl.CostEstimate(flops=5_000_000, bytes_accessed=10_000_000, transcendentals=0),
        name="slots",
    )(tab, shard, theirs)


def row_slots_kernel(tab, mine, theirs, out):
    nz, pair, _, rows, width = out.shape
    zero = jnp.zeros((rows, width), out.dtype)
    for k in range(pair):
        for z in range(nz - 1):
            at = slice(z * rows, (z + 1) * rows), slice(k * width, (k + 1) * width)
            for s, (own, other) in enumerate(((MINE_A, THEIRS_A), (MINE_B, THEIRS_B))):
                out[z, k, s] = jnp.where(
                    tab[own] == 1, mine[at], jnp.where(tab[other] == 1, theirs[at], zero)
                )
        for s in range(2):
            out[nz - 1, k, s] = zero


def build_row_slots(tab, shard, theirs):
    half, width = shard.shape[0] // 2, shard.shape[1] // NK
    rows = half // (NZ - 1)
    return pl.pallas_call(
        row_slots_kernel,
        grid_spec=pltpu.PrefetchScalarGridSpec(
            num_scalar_prefetch=1,
            grid=(NK // PAIR,),
            in_specs=[
                pl.BlockSpec((half, PAIR * width), lambda j, tab: (tab[CORE], j)),
                pl.BlockSpec((half, PAIR * width), lambda j, tab: (0, j)),
            ],
            out_specs=pl.BlockSpec((NZ, PAIR, 2, rows, width), lambda j, tab: (0, j, 0, 0, 0)),
        ),
        out_shape=jax.ShapeDtypeStruct((NZ, NK, 2, rows, width), shard.dtype),
        compiler_params=params(),
        cost_estimate=pl.CostEstimate(flops=5_000_000, bytes_accessed=10_000_000, transcendentals=0),
        name="row_slots",
    )(tab, shard, theirs)


def copy_kernel(x, out):
    width = out.shape[2]
    for k in range(out.shape[0]):
        out[k] = x[:, k * width : (k + 1) * width]


def column_blocks(shard):
    rows, width = shard.shape[0], shard.shape[1] // NK
    return pl.pallas_call(
        copy_kernel,
        grid=(NK // 2,),
        in_specs=[pl.BlockSpec((rows, 2 * width), lambda j: (0, j))],
        out_specs=pl.BlockSpec((2, rows, width), lambda j: (j, 0, 0)),
        out_shape=jax.ShapeDtypeStruct((NK, rows, width), shard.dtype),
        compiler_params=params(),
        cost_estimate=pl.CostEstimate(flops=1_000_000, bytes_accessed=6_400_000, transcendentals=0),
        name="column_blocks",
    )(shard)


def final_kernel(tab, rate, own, gathered, received, back, out):
    half, width = received.shape[1:]
    scale = 0.9 * rate[0]
    loser, first = tab[LOSER] == 1, tab[CORE] == 0

    def rows_of(at, low):
        def body(i, carry):
            here = pl.ds(pl.multiple_of(i * ROWS, ROWS), ROWS)
            there = pl.ds(pl.multiple_of(at + i * ROWS, ROWS), ROWS)
            for j in range(PAIR):
                at_j = pl.ds(j * width, width)
                g, r = gathered[j, 0, here], received[j, here]
                m = jnp.where(loser, jnp.where(low, g, r), own[there, at_j]).astype(jnp.float32)
                out[there, at_j] = (back[j, there].astype(jnp.float32) - scale * m).astype(out.dtype)
            return carry

        lax.fori_loop(0, half // ROWS, body, 0, unroll=True)

    rows_of(0, first)
    rows_of(half, jnp.logical_not(first))


def final(tab, rate, shard, gathered, received, back):
    rows, width = shard.shape[0], shard.shape[1] // NZ
    half = rows // 2
    return pl.pallas_call(
        final_kernel,
        grid_spec=pltpu.PrefetchScalarGridSpec(
            num_scalar_prefetch=2,
            grid=(NZ // PAIR,),
            in_specs=[
                pl.BlockSpec((rows, PAIR * width), lambda j, tab, rate: (0, j)),
                pl.BlockSpec((PAIR, 1, half, width), lambda j, tab, rate: (j, tab[SLOT], 0, 0)),
                pl.BlockSpec((PAIR, half, width), lambda j, tab, rate: (j, 0, 0)),
                pl.BlockSpec((PAIR, rows, width), lambda j, tab, rate: (j, 0, 0)),
            ],
            out_specs=pl.BlockSpec((rows, PAIR * width), lambda j, tab, rate: (0, j)),
        ),
        out_shape=jax.ShapeDtypeStruct(shard.shape, shard.dtype),
        compiler_params=params(),
        cost_estimate=pl.CostEstimate(flops=5_000_000, bytes_accessed=13_000_000, transcendentals=0),
        name="final",
    )(tab, rate, shard, gathered, received, back)


def step_kernel(tab, rate, tokens, own, cot, received, *refs):
    gathered, (act, back, acc, grad, weight) = refs[: len(DISTANCES)], refs[len(DISTANCES) :]
    i = pl.program_id(0)
    steps = NK // PAIR
    pair = lax.rem(i, steps) * PAIR
    half = own.shape[1] // 2
    width = own.shape[2]

    @pl.when(i < steps)
    def _():
        weight[pl.ds(pair, PAIR)] = own[...]
        for n, distance in enumerate(DISTANCES):
            plane = lax.rem(tab[PLANE] + NZ + distance, NZ)

            @pl.when((tab[LOSER] == 1) & (plane < NZ - 1))
            def _():
                near = pl.multiple_of(tab[CORE] * half + plane * ROWS, ROWS)
                far = pl.multiple_of((1 - tab[CORE]) * half + plane * ROWS, ROWS)
                for p in range(PAIR):
                    weight[pair + p, pl.ds(near, ROWS)] = gathered[n][p, 0]
                    weight[pair + p, pl.ds(far, ROWS)] = received[n, p]

        t = tokens[pl.ds(pair, PAIR)].reshape(PAIR * 2 * half, -1)
        w = weight[pl.ds(pair, PAIR)].reshape(PAIR * 2 * half, width)
        part = lax.dot_general(t, w, (((0,), (0,)), ((), ())), preferred_element_type=jnp.float32)

        @pl.when(i == 0)
        def _():
            acc[...] = part

        @pl.when(i > 0)
        def _():
            acc[...] += part

    @pl.when(i == steps - 1)
    def _():
        def body(c, carry):
            rows = pl.ds(pl.multiple_of(c * ROWS, ROWS), ROWS)
            v = acc[rows]
            vv = v * v
            t = jnp.tanh(v * (GELU_A + (GELU_A * GELU_B) * vv))
            up = 0.5 + 0.5 * t
            act[rows] = (v * up).astype(act.dtype)
            slope = up + v * (1.0 - t * t) * (0.5 * GELU_A + (1.5 * GELU_A * GELU_B) * vv)
            grad[rows] = (cot[rows].astype(jnp.float32) * slope).astype(grad.dtype)
            return carry

        lax.fori_loop(0, acc.shape[0] // ROWS, body, 0, unroll=2)

    @pl.when(i >= steps)
    def _():
        t = tokens[pl.ds(pair, PAIR)].reshape(PAIR * 2 * half, -1)
        gw = jnp.dot(t, grad[...], preferred_element_type=jnp.float32)
        w = weight[pl.ds(pair, PAIR)].reshape(PAIR * 2 * half, width)
        back[...] = (w.astype(jnp.float32) - rate[0] * gw).astype(back.dtype).reshape(back.shape)


def step(tab, rate, tokens, own, cot, received, gathered):
    nk, r, t = tokens.shape
    f = own.shape[2]
    pieces, rows = received.shape[0], received.shape[2]
    steps = NK // PAIR

    def at(i):
        return jnp.minimum(i, steps - 1)

    return pl.pallas_call(
        step_kernel,
        grid_spec=pltpu.PrefetchScalarGridSpec(
            num_scalar_prefetch=2,
            grid=(2 * steps,),
            in_specs=[
                pl.BlockSpec((nk, r, t), lambda i, tab, rate: (0, 0, 0)),
                pl.BlockSpec((PAIR, r, f), lambda i, tab, rate: (at(i), 0, 0)),
                pl.BlockSpec((t, f), lambda i, tab, rate: (0, 0)),
                pl.BlockSpec((pieces, PAIR, rows, f), lambda i, tab, rate: (0, at(i), 0, 0)),
            ]
            + [pl.BlockSpec((PAIR, 1, rows, f), lambda i, tab, rate: (at(i), tab[SLOT], 0, 0))] * pieces,
            out_specs=[
                pl.BlockSpec((t, f), lambda i, tab, rate: (0, 0)),
                pl.BlockSpec((PAIR, r, f), lambda i, tab, rate: (jnp.maximum(i - steps, 0), 0, 0)),
            ],
            scratch_shapes=[
                pltpu.VMEM((t, f), jnp.float32),
                pltpu.VMEM((t, f), jnp.bfloat16),
                pltpu.VMEM((nk, r, f), jnp.bfloat16),
            ],
        ),
        out_shape=[
            jax.ShapeDtypeStruct((t, f), jnp.bfloat16),
            jax.ShapeDtypeStruct((nk, r, f), jnp.bfloat16),
        ],
        compiler_params=params(),
        cost_estimate=pl.CostEstimate(
            flops=4 * nk * t * r * f, bytes_accessed=20_000_000, transcendentals=t * f
        ),
        name="step",
    )(tab, rate, tokens, own, cot, received, *gathered)


def swap_core(x):
    return lax.ppermute(x, "c", [(0, 1), (1, 0)])


def swap_column(x):
    return lax.ppermute(x, "yl", [(0, 1), (1, 0)])


def partner_rows(shard, core):
    half = shard.shape[0] // 2
    return swap_core(lax.dynamic_slice_in_dim(shard, (1 - core) * half, half, axis=0))


def scatter(slots):
    return lax.psum_scatter(slots, "z", scatter_dimension=0, tiled=True)


def gather(mine):
    return lax.all_gather(mine, "z", axis=0, tiled=True)


def ring(piece):
    up = [(z, (z + 1) % NZ) for z in range(NZ)]
    down = [(z, (z - 1) % NZ) for z in range(NZ)]
    low = high = piece
    pieces = [piece]
    for _ in range(NZ // 2 - 1):
        low, high = lax.ppermute(low, "z", up), lax.ppermute(high, "z", down)
        pieces += [low, high]
    half = piece.shape[0] // 2
    last = lax.ppermute(low[:half], "z", up), lax.ppermute(high[half:], "z", down)
    return pieces + [jnp.concatenate(last)]


def local(tokens, weight, momentum, cotangent, assignment, lr_index, rates):
    core = lax.axis_index("c")
    me = lax.axis_index(POP)
    partner = me + 1 - 2 * core
    loser_ids, winner_ids = assignment[:, 0], assignment[:, 1]
    win_a, win_b = jnp.min(winner_ids), jnp.max(winner_ids)

    def slot_of(member):
        hit = loser_ids == member
        return jnp.any(hit), jnp.any(hit & (winner_ids == win_b)).astype(jnp.int32)

    loser, slot = slot_of(me)
    _, partner_slot = slot_of(partner)
    tab = jnp.stack(
        [
            (win_a == me).astype(jnp.int32),
            (win_b == me).astype(jnp.int32),
            (win_a == partner).astype(jnp.int32),
            (win_b == partner).astype(jnp.int32),
            core.astype(jnp.int32),
            loser.astype(jnp.int32),
            slot,
            lax.axis_index("z").astype(jnp.int32),
        ]
    )
    member_ids = jnp.arange(lr_index.shape[0], dtype=jnp.int32)
    my_index = jnp.sum(jnp.where(member_ids == me, lr_index, 0))
    rate_ids = jnp.arange(rates.shape[0], dtype=jnp.int32)
    rate = jnp.sum(jnp.where(rate_ids == my_index, rates, 0.0)).reshape(1)

    w, m = weight[0], momentum[0]
    w_slots = build_row_slots(tab, w, partner_rows(w, core))
    w_mine = scatter(w_slots)
    own_columns = lax.all_to_all(column_blocks(w), TP, 0, 0, tiled=True)
    m_slots = build_slots(tab, m, partner_rows(m, core))
    w_mine, own_columns, m_slots = lax.optimization_barrier((w_mine, own_columns, m_slots))
    m_mine = scatter(m_slots)
    both = jnp.broadcast_to(w_mine, (2,) + w_mine.shape[1:])
    both = both.reshape((2 * NK,) + w_mine.shape[2:])
    both = lax.all_to_all(both, ("yl",) + TP, 0, 0, tiled=True)
    w_mine = both[:NK] + both[NK:]
    turned = jnp.swapaxes(tokens, 1, 2)
    w_mine, turned = lax.optimization_barrier((w_mine, turned))
    all_tokens = lax.all_to_all(
        jnp.broadcast_to(turned, (NK,) + turned.shape[1:]), TP, 0, 0, tiled=True
    )
    pieces = ring(w_mine)
    pieces[-1], m_mine, all_tokens = lax.optimization_barrier((pieces[-1], m_mine, all_tokens))
    w_other = swap_core(
        jnp.stack(
            [lax.dynamic_index_in_dim(p, partner_slot, axis=1, keepdims=False) for p in pieces]
        )
    )
    m_across, w_other = lax.optimization_barrier((swap_column(m_mine), w_other))
    m_won = gather(m_mine + m_across)
    activation, back = step(tab, rate, all_tokens, own_columns, cotangent[0], w_other, pieces)
    back = lax.all_to_all(back, TP, 0, 0, tiled=True)
    m_other = swap_core(lax.dynamic_index_in_dim(m_won, partner_slot, axis=1, keepdims=False))
    updated = final(tab, rate, m, m_won, m_other, back)
    return (activation[None], updated[None])


def solution(mesh):
    fine = Mesh(mesh.devices.reshape(8, 2, 2, 2, 4), POP + TP)
    placed = (
        P(POP, None, TP),
        P(POP, TP, None),
        P(POP, TP, None),
        P(POP, None, TP),
        P(),
        P(),
        P(),
    )
    return jax.shard_map(
        local,
        mesh=fine,
        in_specs=placed,
        out_specs=(P(POP, None, TP), P(POP, TP, None)),
        check_vma=False,
    )
```

time: 279 us -> 268 us (0.961)
  blocking collectives: 78 us -> 19.7 us
  starting transfers between devices: 9.63 us -> 40.2 us
  waiting for transfers between devices: 115 us -> 138 us
  Pallas kernels: 42.8 us -> 32.2 us
  local copies, waits for them, and re-layouts: 6.72 us -> 13.2 us
    all_to_all x2 -> x1, blocking collectives: 78 us -> 19.7 us  [local(): both = lax.all_to_all(both, ('yl',) + TP, 0, 0, tiled=True)]
    all_to_all x0 -> x2, waiting for transfers between devices: none -> 39.7 us  [the longest x1 39.7 us: local(): own_columns = lax.all_to_all(column_blocks(w), TP, 0, 0, tiled=True)]
    ppermute x2 -> x9, waiting for transfers between devices: 16.6 us -> 52.3 us  [the longest x6 34.8 us: ring(): low, high = (lax.ppermute(low, 'z', up), lax.ppermute(high, 'z', down))]
    all_gather x2 -> x1, waiting for transfers between devices: 51.9 us -> 19.3 us  [gather(): return lax.all_gather(mine, 'z', axis=0, tiled=True)]
    reduce_scatter x2, waiting for transfers between devices: 17.7 us -> 0.02 us  [scatter(): return lax.psum_scatter(slots, 'z', scatter_dimension=0, tiled=True)]
    ppermute x2 -> x9, starting transfers between devices: 2.14 us -> 18.3 us  [the longest x6 12.9 us: ring(): low, high = (lax.ppermute(low, 'z', up), lax.ppermute(high, 'z', down))]
    all_to_all x0 -> x2, starting transfers between devices: none -> 14.4 us  [the longest x1 7.67 us: local(): own_columns = lax.all_to_all(column_blocks(w), TP, 0, 0, tiled=True)]
    pallas_call x2 -> x1, Pallas kernels: 12.9 us -> 4.55 us  [build_slots(): pl.pallas_call(slots_kernel, grid_spec=pltpu.PrefetchScalarGridSpec(num_s...]
  transfers between devices with their start and end apart: 11 -> 19, of which waited for: 8 -> 10; matrix products, arithmetic and copies ran while one was open for 3% -> 3% of each run, Pallas kernels for 10% -> 8%
where the time goes in v2:
time: 268 us
  waiting for transfers between devices  138 us (51%)
  starting transfers between devices  40.2 us (15%)
  Pallas kernels  32.2 us (12%)
  blocking collectives  19.7 us (7%)
  between operations  18.6 us (7%)
  local copies, waits for them, and re-layouts  13.2 us (5%)
  other arithmetic  6.07 us (2%)
    all_to_all x1, waiting for transfers between devices, local(): own_columns = lax.all_to_all(column_blocks(w), TP, 0, 0, tiled=True)  39.7 us
    ppermute x6, waiting for transfers between devices, ring(): low, high = (lax.ppermute(low, 'z', up), lax.ppermute(high, 'z', down))  34.8 us
    all_to_all x1, waiting for transfers between devices, local(): back = lax.all_to_all(back, TP, 0, 0, tiled=True)  23.2 us
    all_to_all x1, blocking collectives, local(): both = lax.all_to_all(both, ('yl',) + TP, 0, 0, tiled=True)  19.7 us
    all_gather x1, waiting for transfers between devices, gather(): return lax.all_gather(mine, 'z', axis=0, tiled=True)  19.3 us
    pallas_call x1, Pallas kernels, step(): pl.pallas_call(step_kernel, grid_spec=pltpu.PrefetchScalarGridSpec(num_sc...  13.5 us
    ppermute x6, starting transfers between devices, ring(): low, high = (lax.ppermute(low, 'z', up), lax.ppermute(high, 'z', down))  12.9 us
    ppermute x1, waiting for transfers between devices, swap_column(): return lax.ppermute(x, 'yl', [(0, 1), (1, 0)])  10.4 us
  transfers between devices with their start and end apart: 19, of which 10 were waited for; matrix products, arithmetic and copies ran while one was open for 3% of the time, Pallas kernels for 8%

profile of v2, /device:TPU:6, one launch (start us, length us, event | category | flops | bytes accessed | tf_op | source)
XLA Modules:
  0.0 267.9 jit_solution(14653600631453607465)
XLA Ops:
  7.2 2.8 %dynamic-slice_bitcast_fusion.2 = bf16[112,7168]{1,0:T(8,128)(2,1)} fusion(bf16[1,224,7168]{2,1,0:T(8,128)(2,1)} %param.8, s32[]{:T(128)S(6)} %select_n.27), kind=kLoop, calls=%fused_computation.2 | loop fusion | bytes 3211268 | tf_op jit(solution)/shard_map/dynamic_slice | solution.py:268
  16.3 4.7 %row_slots.1 = bf16[8,8,2,16,896]{4,3,2,1,0:T(8,128)(2,1)} custom-call(s32[8]{0:T(128)S(1)} %stack.86.tab, bf16[224,7168]{1,0:T(8,128)(2,1)S(1)} %bitcast.43, bf16[112,7168]{1,0:T(8,128)(2,1)} %collective-permute-done.theirs), custom_call_target="tpu_custom_call" | custom-call | flops 5000000 | bytes 10000000 | tf_op jit(solution)/shard_map/row_slots/pallas_call | solution.py:75
  25.5 7.7 %all-to-all-start = ((bf16[8,224,896]{2,1,0:T(8,128)(2,1)}), bf16[8,224,896]{2,1,0:T(8,128)(2,1)}, u32[]{:S(2)}, u32[]{:S(2)}) async-start(bf16[8,224,896]{2,1,0:T(8,128)(2,1)} %copy-done.3), calls=%async_computation.1 | async-start | bytes 6422528 | tf_op jit(solution)/shard_map/all_to_all | solution.py:325
  33.4 3.4 %collective-permute-done.1.theirs = bf16[112,7168]{1,0:T(8,128)(2,1)S(1)} collective-permute-done((bf16[112,7168]{1,0:T(8,128)(2,1)S(1)}, bf16[112,7168]{1,0:T(8,128)(2,1)S(1)}, u32[]{:S(2)}, u32[]{:S(2)}) %collective-permute-start.1) | collective-permute-done | bytes 1605664 | tf_op jit(solution)/shard_map/ppermute | solution.py:259
  36.8 4.5 %slots.1 = bf16[8,2,112,896]{3,2,1,0:T(8,128)(2,1)} custom-call(s32[8]{0:T(128)S(1)} %stack.86.tab, bf16[224,7168]{1,0:T(8,128)(2,1)} %bitcast.40, bf16[112,7168]{1,0:T(8,128)(2,1)S(1)} %collective-permute-done.1.theirs), custom_call_target="tpu_custom_call" | custom-call | flops 5000000 | bytes 10000000 | tf_op jit(solution)/shard_map/slots/pallas_call | solution.py:40
  41.3 39.7 %all-to-all-done.own = bf16[8,224,896]{2,1,0:T(8,128)(2,1)} async-done(((bf16[8,224,896]{2,1,0:T(8,128)(2,1)}), bf16[8,224,896]{2,1,0:T(8,128)(2,1)}, u32[]{:S(2)}, u32[]{:S(2)}) %all-to-all-start) | async-done | bytes 3211296 | tf_op jit(solution)/shard_map/all_to_all | solution.py:325
  82.1 19.7 %all_to_all.20 = bf16[16,2,16,896]{3,2,1,0:T(8,128)(2,1)S(1)} all-to-all(bf16[16,2,16,896]{3,2,1,0:T(8,128)(2,1)S(1)} %bitcast.45), channel_id=1, replica_groups=mesh['z'=8,'yl'=2,'c'=2,'yh'=2,'x'=4] {'yl','yh','x'}, dimensions={0} | all-to-all | bytes 1835008 | tf_op jit(solution)/shard_map/all_to_all | solution.py:331
  101.9 5.9 %collective-permute-start.6 = (bf16[8,2,16,896]{3,2,1,0:T(8,128)(2,1)S(1)}, bf16[8,2,16,896]{3,2,1,0:T(8,128)(2,1)S(1)}, u32[]{:S(2)}, u32[]{:S(2)}) collective-permute-start(bf16[8,2,16,896]{3,2,1,0:T(8,128)(2,1)S(1)} %slice_add_fusion.refs_0_), channel_id=1, source_target_pairs={{0,224},{32,0},{64,32},{96,64},{128,96},{160,128},{192,160},{224,1... | collective-permute-start | bytes 1376264 | tf_op jit(solution)/shard_map/ppermute | solution.py:285
  109.2 6.7 %all-to-all-start.2 = ((bf16[8,224,512]{2,1,0:T(8,128)(2,1)}), bf16[8,224,512]{2,1,0:T(8,128)(2,1)}, u32[]{:S(2)}, u32[]{:S(2)}) async-start(bf16[8,224,512]{2,1,0:T(8,128)(2,1)} %broadcast_in_dim.33), calls=%async_computation.4 | async-start | bytes 3670016 | tf_op jit(solution)/shard_map/all_to_all | solution.py:335
  115.9 11.6 %collective-permute-done.6.refs_2_ = bf16[8,2,16,896]{3,2,1,0:T(8,128)(2,1)S(1)} collective-permute-done((bf16[8,2,16,896]{3,2,1,0:T(8,128)(2,1)S(1)}, bf16[8,2,16,896]{3,2,1,0:T(8,128)(2,1)S(1)}, u32[]{:S(2)}, u32[]{:S(2)}) %collective-permute-start.6) | collective-permute-done | bytes 458784 | tf_op jit(solution)/shard_map/ppermute | solution.py:285
  127.6 3.7 %collective-permute-start.7 = (bf16[8,2,16,896]{3,2,1,0:T(8,128)(2,1)S(1)}, bf16[8,2,16,896]{3,2,1,0:T(8,128)(2,1)S(1)}, u32[]{:S(2)}, u32[]{:S(2)}) collective-permute-start(bf16[8,2,16,896]{3,2,1,0:T(8,128)(2,1)S(1)} %collective-permute-done.6.refs_2_), channel_id=1, source_target_pairs={{0,224},{32,0},{64,32},{96,64},{128,96},{160,128},{192,160},{224,1... | collective-permute-start | bytes 1376264 | tf_op jit(solution)/shard_map/ppermute | solution.py:285
  131.9 14.5 %collective-permute-done.7.refs_4_ = bf16[8,2,16,896]{3,2,1,0:T(8,128)(2,1)S(1)} collective-permute-done((bf16[8,2,16,896]{3,2,1,0:T(8,128)(2,1)S(1)}, bf16[8,2,16,896]{3,2,1,0:T(8,128)(2,1)S(1)}, u32[]{:S(2)}, u32[]{:S(2)}) %collective-permute-start.7) | collective-permute-done | bytes 458784 | tf_op jit(solution)/shard_map/ppermute | solution.py:285
  146.5 3.3 %collective-permute-start.8 = (bf16[8,2,16,896]{3,2,1,0:T(8,128)(2,1)S(1)}, bf16[8,2,16,896]{3,2,1,0:T(8,128)(2,1)S(1)}, u32[]{:S(2)}, u32[]{:S(2)}) collective-permute-start(bf16[8,2,16,896]{3,2,1,0:T(8,128)(2,1)S(1)} %collective-permute-done.7.refs_4_), channel_id=1, source_target_pairs={{0,224},{32,0},{64,32},{96,64},{128,96},{160,128},{192,160},{224,1... | collective-permute-start | bytes 1376264 | tf_op jit(solution)/shard_map/ppermute | solution.py:285
  149.9 8.7 %collective-permute-done.8.refs_6_ = bf16[8,2,16,896]{3,2,1,0:T(8,128)(2,1)S(1)} collective-permute-done((bf16[8,2,16,896]{3,2,1,0:T(8,128)(2,1)S(1)}, bf16[8,2,16,896]{3,2,1,0:T(8,128)(2,1)S(1)}, u32[]{:S(2)}, u32[]{:S(2)}) %collective-permute-start.8) | collective-permute-done | bytes 458784 | tf_op jit(solution)/shard_map/ppermute | solution.py:285
  158.6 3.8 %collective-permute-start.9 = (bf16[4,2,16,896]{3,2,1,0:T(8,128)(2,1)S(1)}, bf16[4,2,16,896]{3,2,1,0:T(8,128)(2,1)S(1)}, u32[]{:S(2)}, u32[]{:S(2)}) collective-permute-start(bf16[4,2,16,896]{3,2,1,0:T(8,128)(2,1)S(1)} %slice.27), channel_id=1, source_target_pairs={{0,224},{32,0},{64,32},{96,64},{128,96},{160,128},{192,160},{224,1... | collective-permute-start | bytes 688136 | tf_op jit(solution)/shard_map/ppermute | solution.py:288
  162.6 3.3 %collective-permute-done.9 = bf16[4,2,16,896]{3,2,1,0:T(8,128)(2,1)S(1)} collective-permute-done((bf16[4,2,16,896]{3,2,1,0:T(8,128)(2,1)S(1)}, bf16[4,2,16,896]{3,2,1,0:T(8,128)(2,1)S(1)}, u32[]{:S(2)}, u32[]{:S(2)}) %collective-permute-start.9) | collective-permute-done | bytes 229408 | tf_op jit(solution)/shard_map/ppermute | solution.py:288
  165.9 3.8 %collective-permute-done.5 = bf16[4,2,16,896]{3,2,1,0:T(8,128)(2,1)S(1)} collective-permute-done((bf16[4,2,16,896]{3,2,1,0:T(8,128)(2,1)S(1)}, bf16[4,2,16,896]{3,2,1,0:T(8,128)(2,1)S(1)}, u32[]{:S(2)}, u32[]{:S(2)}) %collective-permute-start.5) | collective-permute-done | bytes 229408 | tf_op jit(solution)/shard_map/ppermute | solution.py:288
  172.0 10.4 %collective-permute-done.10 = bf16[1,2,112,896]{3,2,1,0:T(8,128)(2,1)S(1)} collective-permute-done((bf16[1,2,112,896]{3,2,1,0:T(8,128)(2,1)}, bf16[1,2,112,896]{3,2,1,0:T(8,128)(2,1)S(1)}, u32[]{:S(2)}, u32[]{:S(2)}) %collective-permute-start.10) | collective-permute-done | bytes 401440 | tf_op jit(solution)/shard_map/ppermute | solution.py:263
  188.5 13.5 %step.1 = (bf16[512,896]{1,0:T(8,128)(2,1)}, bf16[8,224,896]{2,1,0:T(8,128)(2,1)}) custom-call(s32[8]{0:T(128)S(1)} %stack.86.tab, f32[1]{0:T(128)} %bitcast.8.rate, bf16[8,224,512]{2,1,0:T(8,128)(2,1)} %all-to-all-done.2.tokens, bf16[8,224,896]{2,1,0:T(8,128)(2,1)} %all-to-all-done.own, bf16[512,896]{1,0:T(8,128)(2,1)S(1)} %bitcast.44, ...), custom_call_target="tpu_custom_call" | custom-call | flops 3288334336 | bytes 20000000 | tf_op jit(solution)/shard_map/step/pallas_call | solution.py:224
  202.1 7.4 %all-to-all-start.3 = ((bf16[8,224,896]{2,1,0:T(8,128)(2,1)}), bf16[8,224,896]{2,1,0:T(8,128)(2,1)}, u32[]{:S(2)}, u32[]{:S(2)}) async-start(bf16[8,224,896]{2,1,0:T(8,128)(2,1)} %get-tuple-element.25), calls=%async_computation.5 | async-start | bytes 6422528 | tf_op jit(solution)/shard_map/all_to_all | solution.py:348
  209.5 19.3 %all-gather.2.cloned.1.call-done.gathered = bf16[8,2,112,896]{3,2,1,0:T(8,128)(2,1)} async-done(((bf16[1,2,112,896]{3,2,1,0:T(8,128)(2,1)}), bf16[8,2,112,896]{3,2,1,0:T(8,128)(2,1)}) %all-gather.2.cloned.1.call-update) | async-done | bytes 3211280 | tf_op jit(solution)/shard_map/all_gather | solution.py:276
  228.7 2.8 %dynamic-slice_bitcast_fusion = bf16[8,112,896]{2,1,0:T(8,128)(2,1)} fusion(bf16[8,2,112,896]{3,2,1,0:T(8,128)(2,1)} %all-gather.2.cloned.1.call-done.gathered, s32[]{:T(128)S(6)} %select_n.28), kind=kLoop, calls=%fused_computation | loop fusion | bytes 3211268 | tf_op jit(solution)/shard_map/jit(dynamic_index_in_dim)/squeeze | solution.py:349
  231.5 23.2 %all-to-all-done.3.back = bf16[8,224,896]{2,1,0:T(8,128)(2,1)} async-done(((bf16[8,224,896]{2,1,0:T(8,128)(2,1)}), bf16[8,224,896]{2,1,0:T(8,128)(2,1)}, u32[]{:S(2)}, u32[]{:S(2)}) %all-to-all-start.3) | async-done | bytes 3211296 | tf_op jit(solution)/shard_map/all_to_all | solution.py:348
  254.7 6.7 %final.1 = bf16[224,7168]{1,0:T(8,128)(2,1)} custom-call(s32[8]{0:T(128)S(1)} %stack.86.tab, f32[1]{0:T(128)} %bitcast.8.rate, bf16[224,7168]{1,0:T(8,128)(2,1)S(1)} %bitcast.41, bf16[8,2,112,896]{3,2,1,0:T(8,128)(2,1)} %all-gather.2.cloned.1.call-done.gathered, bf16[8,112,896]{2,1,0:T(8,128)(2,1)} %collective-permute-done.12.received, ...), custom_call_target="tpu_custom_call" | custom-call | flops 5000000 | bytes 13000000 | tf_op jit(solution)/shard_map/final/pallas_call | solution.py:138
  (72 shorter events, 18.2 us)
Async XLA Ops:
  7.2 73.8 %reduce-scatter.3.cloned.1.call-start = ((), (), s32[]{:S(2)}) async-start(), calls=%async_computation.6 | async-start | bytes 4128768 | tf_op jit(solution)/shard_map/reduce_scatter | solution.py:272
  10.1 6.2 %collective-permute-start = (bf16[112,7168]{1,0:T(8,128)(2,1)}, bf16[112,7168]{1,0:T(8,128)(2,1)}, u32[]{:S(2)}, u32[]{:S(2)}) collective-permute-start(bf16[112,7168]{1,0:T(8,128)(2,1)} %dynamic-slice_bitcast_fusion.2), channel_id=1, source_target_pairs={{0,8},{8,0},{1,9},{9,1},{2,10},{10,2},{3,11},{11,3},{4,12},{12,4},... | collective-permute-start | bytes 4816904 | tf_op jit(solution)/shard_map/ppermute | solution.py:259
  25.5 55.6 %all-to-all-start = ((bf16[8,224,896]{2,1,0:T(8,128)(2,1)}), bf16[8,224,896]{2,1,0:T(8,128)(2,1)}, u32[]{:S(2)}, u32[]{:S(2)}) async-start(bf16[8,224,896]{2,1,0:T(8,128)(2,1)} %copy-done.3), calls=%async_computation.1 | async-start | bytes 6422528 | tf_op jit(solution)/shard_map/all_to_all | solution.py:325
  33.1 136.7 %reduce-scatter.5.cloned.1.call-start = ((), (), s32[]{:S(2)}) async-start(), calls=%async_computation.7 | async-start | bytes 3612672 | tf_op jit(solution)/shard_map/reduce_scatter | solution.py:272
  33.3 3.5 %collective-permute-start.1 = (bf16[112,7168]{1,0:T(8,128)(2,1)S(1)}, bf16[112,7168]{1,0:T(8,128)(2,1)S(1)}, u32[]{:S(2)}, u32[]{:S(2)}) collective-permute-start(bf16[112,7168]{1,0:T(8,128)(2,1)S(1)} %dynamic-slice_bitcast_fusion.1), channel_id=1, source_target_pairs={{0,8},{8,0},{1,9},{9,1},{2,10},{10,2},{3,11},{11,3},{4,12},{12,4},... | collective-permute-start | bytes 4816904 | tf_op jit(solution)/shard_map/ppermute | solution.py:259
  82.1 25.7 %copy-start.8 = (bf16[1,512,224]{1,2,0:T(8,128)(2,1)S(1)}, bf16[1,512,224]{1,2,0:T(8,128)(2,1)}, u32[]{:S(2)}) copy-start(bf16[1,512,224]{1,2,0:T(8,128)(2,1)} %param.7) | copy-start | bytes 688132
  101.9 25.7 %collective-permute-start.6 = (bf16[8,2,16,896]{3,2,1,0:T(8,128)(2,1)S(1)}, bf16[8,2,16,896]{3,2,1,0:T(8,128)(2,1)S(1)}, u32[]{:S(2)}, u32[]{:S(2)}) collective-permute-start(bf16[8,2,16,896]{3,2,1,0:T(8,128)(2,1)S(1)} %slice_add_fusion.refs_0_), channel_id=1, source_target_pairs={{0,224},{32,0},{64,32},{96,64},{128,96},{160,128},{192,160},{224,1... | collective-permute-start | bytes 1376264 | tf_op jit(solution)/shard_map/ppermute | solution.py:285
  107.8 23.4 %collective-permute-start.2 = (bf16[8,2,16,896]{3,2,1,0:T(8,128)(2,1)S(1)}, bf16[8,2,16,896]{3,2,1,0:T(8,128)(2,1)S(1)}, u32[]{:S(2)}, u32[]{:S(2)}) collective-permute-start(bf16[8,2,16,896]{3,2,1,0:T(8,128)(2,1)S(1)} %slice_add_fusion.refs_0_), channel_id=1, source_target_pairs={{0,32},{32,64},{64,96},{96,128},{128,160},{160,192},{192,224},{224... | collective-permute-start | bytes 1376264 | tf_op jit(solution)/shard_map/ppermute | solution.py:285
  109.2 60.6 %all-to-all-start.2 = ((bf16[8,224,512]{2,1,0:T(8,128)(2,1)}), bf16[8,224,512]{2,1,0:T(8,128)(2,1)}, u32[]{:S(2)}, u32[]{:S(2)}) async-start(bf16[8,224,512]{2,1,0:T(8,128)(2,1)} %broadcast_in_dim.33), calls=%async_computation.4 | async-start | bytes 3670016 | tf_op jit(solution)/shard_map/all_to_all | solution.py:335
  115.9 112.8 %all-gather.2.cloned.1.call-start = ((), (), s32[]{:S(2)}) async-start(), calls=%async_computation.8 | async-start | bytes 3612672 | tf_op jit(solution)/shard_map/all_gather | solution.py:276
  127.6 18.9 %collective-permute-start.7 = (bf16[8,2,16,896]{3,2,1,0:T(8,128)(2,1)S(1)}, bf16[8,2,16,896]{3,2,1,0:T(8,128)(2,1)S(1)}, u32[]{:S(2)}, u32[]{:S(2)}) collective-permute-start(bf16[8,2,16,896]{3,2,1,0:T(8,128)(2,1)S(1)} %collective-permute-done.6.refs_2_), channel_id=1, source_target_pairs={{0,224},{32,0},{64,32},{96,64},{128,96},{160,128},{192,160},{224,1... | collective-permute-start | bytes 1376264 | tf_op jit(solution)/shard_map/ppermute | solution.py:285
  131.3 18.5 %collective-permute-start.3 = (bf16[8,2,16,896]{3,2,1,0:T(8,128)(2,1)S(1)}, bf16[8,2,16,896]{3,2,1,0:T(8,128)(2,1)S(1)}, u32[]{:S(2)}, u32[]{:S(2)}) collective-permute-start(bf16[8,2,16,896]{3,2,1,0:T(8,128)(2,1)S(1)} %collective-permute-done.2.refs_1_), channel_id=1, source_target_pairs={{0,32},{32,64},{64,96},{96,128},{128,160},{160,192},{192,224},{224... | collective-permute-start | bytes 1376264 | tf_op jit(solution)/shard_map/ppermute | solution.py:285
  146.5 12.1 %collective-permute-start.8 = (bf16[8,2,16,896]{3,2,1,0:T(8,128)(2,1)S(1)}, bf16[8,2,16,896]{3,2,1,0:T(8,128)(2,1)S(1)}, u32[]{:S(2)}, u32[]{:S(2)}) collective-permute-start(bf16[8,2,16,896]{3,2,1,0:T(8,128)(2,1)S(1)} %collective-permute-done.7.refs_4_), channel_id=1, source_target_pairs={{0,224},{32,0},{64,32},{96,64},{128,96},{160,128},{192,160},{224,1... | collective-permute-start | bytes 1376264 | tf_op jit(solution)/shard_map/ppermute | solution.py:285
  149.8 12.8 %copy-start.4 = (bf16[8,2,16,896]{3,2,1,0:T(8,128)(2,1)}, bf16[8,2,16,896]{3,2,1,0:T(8,128)(2,1)S(1)}, u32[]{:S(2)}) copy-start(bf16[8,2,16,896]{3,2,1,0:T(8,128)(2,1)S(1)} %collective-permute-done.3.refs_3_) | copy-start | bytes 1376260
  149.8 12.6 %collective-permute-start.4 = (bf16[8,2,16,896]{3,2,1,0:T(8,128)(2,1)S(1)}, bf16[8,2,16,896]{3,2,1,0:T(8,128)(2,1)S(1)}, u32[]{:S(2)}, u32[]{:S(2)}) collective-permute-start(bf16[8,2,16,896]{3,2,1,0:T(8,128)(2,1)S(1)} %collective-permute-done.3.refs_3_), channel_id=1, source_target_pairs={{0,32},{32,64},{64,96},{96,128},{128,160},{160,192},{192,224},{224... | collective-permute-start | bytes 1376264 | tf_op jit(solution)/shard_map/ppermute | solution.py:285
  158.6 7.3 %collective-permute-start.9 = (bf16[4,2,16,896]{3,2,1,0:T(8,128)(2,1)S(1)}, bf16[4,2,16,896]{3,2,1,0:T(8,128)(2,1)S(1)}, u32[]{:S(2)}, u32[]{:S(2)}) collective-permute-start(bf16[4,2,16,896]{3,2,1,0:T(8,128)(2,1)S(1)} %slice.27), channel_id=1, source_target_pairs={{0,224},{32,0},{64,32},{96,64},{128,96},{160,128},{192,160},{224,1... | collective-permute-start | bytes 688136 | tf_op jit(solution)/shard_map/ppermute | solution.py:288
  162.4 7.3 %collective-permute-start.5 = (bf16[4,2,16,896]{3,2,1,0:T(8,128)(2,1)S(1)}, bf16[4,2,16,896]{3,2,1,0:T(8,128)(2,1)S(1)}, u32[]{:S(2)}, u32[]{:S(2)}) collective-permute-start(bf16[4,2,16,896]{3,2,1,0:T(8,128)(2,1)S(1)} %slice.26), channel_id=1, source_target_pairs={{0,32},{32,64},{64,96},{96,128},{128,160},{160,192},{192,224},{224... | collective-permute-start | bytes 688136 | tf_op jit(solution)/shard_map/ppermute | solution.py:288
  162.5 21.8 %copy-start.11 = (s32[32]{0:T(128)S(1)}, s32[32]{0:T(128)}, u32[]{:S(2)}) copy-start(s32[32]{0:T(128)} %param.12) | copy-start | bytes 388
  162.6 22.5 %copy-start.12 = (f32[8]{0:T(128)S(1)}, f32[8]{0:T(128)}, u32[]{:S(2)}) copy-start(f32[8]{0:T(128)} %param.13) | copy-start | bytes 100
  170.5 11.9 %collective-permute-start.11 = (bf16[8,8,16,896]{3,2,1,0:T(8,128)(2,1)}, bf16[8,8,16,896]{3,2,1,0:T(8,128)(2,1)}, u32[]{:S(2)}, u32[]{:S(2)}) collective-permute-start(bf16[8,8,16,896]{3,2,1,0:T(8,128)(2,1)} %bitcast_dynamic-update-slice_fusion), channel_id=1, source_target_pairs={{0,8},{8,0},{1,9},{9,1},{2,10},{10,2},{3,11},{11,3},{4,12},{12,4},... | collective-permute-start | bytes 5505032 | tf_op jit(solution)/shard_map/ppermute | solution.py:259
  170.5 11.9 %collective-permute-start.10 = (bf16[1,2,112,896]{3,2,1,0:T(8,128)(2,1)}, bf16[1,2,112,896]{3,2,1,0:T(8,128)(2,1)S(1)}, u32[]{:S(2)}, u32[]{:S(2)}) collective-permute-start(bf16[1,2,112,896]{3,2,1,0:T(8,128)(2,1)} %reduce-scatter.5.cloned.1.call-done), channel_id=1, source_target_pairs={{0,16},{16,0},{1,17},{17,1},{2,18},{18,2},{3,19},{19,3},{4,20},{20... | collective-permute-start | bytes 1204232 | tf_op jit(solution)/shard_map/ppermute | solution.py:263
  202.1 52.6 %all-to-all-start.3 = ((bf16[8,224,896]{2,1,0:T(8,128)(2,1)}), bf16[8,224,896]{2,1,0:T(8,128)(2,1)}, u32[]{:S(2)}, u32[]{:S(2)}) async-start(bf16[8,224,896]{2,1,0:T(8,128)(2,1)} %get-tuple-element.25), calls=%async_computation.5 | async-start | bytes 6422528 | tf_op jit(solution)/shard_map/all_to_all | solution.py:348
  209.5 45.2 %copy-start.1 = (bf16[1,224,7168]{2,1,0:T(8,128)(2,1)S(1)}, bf16[1,224,7168]{2,1,0:T(8,128)(2,1)}, u32[]{:S(2)}) copy-start(bf16[1,224,7168]{2,1,0:T(8,128)(2,1)} %param.9) | copy-start | bytes 9633796
  231.5 23.2 %collective-permute-start.12 = (bf16[8,112,896]{2,1,0:T(8,128)(2,1)}, bf16[8,112,896]{2,1,0:T(8,128)(2,1)}, u32[]{:S(2)}, u32[]{:S(2)}) collective-permute-start(bf16[8,112,896]{2,1,0:T(8,128)(2,1)} %dynamic-slice_bitcast_fusion), channel_id=1, source_target_pairs={{0,8},{8,0},{1,9},{9,1},{2,10},{10,2},{3,11},{11,3},{4,12},{12,4},... | collective-permute-start | bytes 4816904 | tf_op jit(solution)/shard_map/ppermute | solution.py:259
  (8 other events, 27.9 us)
Sparse Core Ops, SparseCore 0:
  21.1 53.4 reduce-scatter.2
  81.2 65.1 reduce-scatter.4
  184.5 44.1 all-gather.1

commit v3 on v2

--- a/solution.py
+++ b/solution.py
@@ -276,17 +276,19 @@
     return lax.all_gather(mine, "z", axis=0, tiled=True)
 
 
-def ring(piece):
+def ring(piece, behind):
     up = [(z, (z + 1) % NZ) for z in range(NZ)]
     down = [(z, (z - 1) % NZ) for z in range(NZ)]
     low = high = piece
     pieces = [piece]
-    for _ in range(NZ // 2 - 1):
+    for n in range(NZ // 2 - 1):
         low, high = lax.ppermute(low, "z", up), lax.ppermute(high, "z", down)
+        if n == 1:
+            low, high, behind = lax.optimization_barrier((low, high, behind))
         pieces += [low, high]
     half = piece.shape[0] // 2
     last = lax.ppermute(low[:half], "z", up), lax.ppermute(high[half:], "z", down)
-    return pieces + [jnp.concatenate(last)]
+    return pieces + [jnp.concatenate(last)], behind
 
 
 def local(tokens, weight, momentum, cotangent, assignment, lr_index, rates):
@@ -324,7 +326,9 @@
     w_mine = scatter(w_slots)
     own_columns = lax.all_to_all(column_blocks(w), TP, 0, 0, tiled=True)
     m_slots = build_slots(tab, m, partner_rows(m, core))
-    w_mine, own_columns, m_slots = lax.optimization_barrier((w_mine, own_columns, m_slots))
+    w_mine, own_columns, m_slots, rate = lax.optimization_barrier(
+        (w_mine, own_columns, m_slots, rate)
+    )
     m_mine = scatter(m_slots)
     both = jnp.broadcast_to(w_mine, (2,) + w_mine.shape[1:])
     both = both.reshape((2 * NK,) + w_mine.shape[2:])
@@ -335,14 +339,14 @@
     all_tokens = lax.all_to_all(
         jnp.broadcast_to(turned, (NK,) + turned.shape[1:]), TP, 0, 0, tiled=True
     )
-    pieces = ring(w_mine)
-    pieces[-1], m_mine, all_tokens = lax.optimization_barrier((pieces[-1], m_mine, all_tokens))
+    pieces, (m_mine, all_tokens) = ring(w_mine, (m_mine, all_tokens))
+    m_across = swap_column(m_mine)
     w_other = swap_core(
         jnp.stack(
             [lax.dynamic_index_in_dim(p, partner_slot, axis=1, keepdims=False) for p in pieces]
         )
     )
-    m_across, w_other = lax.optimization_barrier((swap_column(m_mine), w_other))
+    m_across, w_other = lax.optimization_barrier((m_across, w_other))
     m_won = gather(m_mine + m_across)
     activation, back = step(tab, rate, all_tokens, own_columns, cotangent[0], w_other, pieces)
     back = lax.all_to_all(back, TP, 0, 0, tiled=True)

time: 268 us -> 263 us (0.981)
  waiting for transfers between devices: 138 us -> 127 us
  local copies, waits for them, and re-layouts: 13.2 us -> 18.3 us
    unnamed x33 -> x34, local copies, waits for them, and re-layouts: 5.15 us -> 10.2 us
    all_to_all x1, waiting for transfers between devices: 23.2 us -> 18.4 us  [local(): back = lax.all_to_all(back, TP, 0, 0, tiled=True)]
    ppermute x1, waiting for transfers between devices: 3.29 us -> 0.01 us  [ring(): lax.ppermute(high[half:], 'z', down)]
    all_gather x1, waiting for transfers between devices: 19.3 us -> 22.3 us  [gather(): return lax.all_gather(mine, 'z', axis=0, tiled=True)]
  transfers between devices with their start and end apart: 19 -> 19, of which waited for: 10 -> 10; matrix products, arithmetic and copies ran while one was open for 3% -> 5% of each run, Pallas kernels for 8% -> 8%
where the time goes in v3:
time: 263 us; the launch traced here: 261 us
  waiting for transfers between devices  127 us (48%)
  starting transfers between devices  39 us (15%)
  Pallas kernels  32.4 us (12%)
  blocking collectives  19.7 us (7%)
  between operations  18.6 us (7%)
  local copies, waits for them, and re-layouts  18.3 us (7%)
  other arithmetic  5.01 us (2%)
    all_to_all x1, waiting for transfers between devices, local(): own_columns = lax.all_to_all(column_blocks(w), TP, 0, 0, tiled=True)  39.6 us
    ppermute x6, waiting for transfers between devices, ring(): low, high = (lax.ppermute(low, 'z', up), lax.ppermute(high, 'z', down))  32.7 us
    all_gather x1, waiting for transfers between devices, gather(): return lax.all_gather(mine, 'z', axis=0, tiled=True)  22.3 us
    all_to_all x1, blocking collectives, local(): both = lax.all_to_all(both, ('yl',) + TP, 0, 0, tiled=True)  19.7 us
    all_to_all x1, waiting for transfers between devices, local(): back = lax.all_to_all(back, TP, 0, 0, tiled=True)  18.4 us
    pallas_call x1, Pallas kernels, step(): pl.pallas_call(step_kernel, grid_spec=pltpu.PrefetchScalarGridSpec(num_sc...  13.8 us
    ppermute x6, starting transfers between devices, ring(): low, high = (lax.ppermute(low, 'z', up), lax.ppermute(high, 'z', down))  12.9 us
    ppermute x1, waiting for transfers between devices, swap_column(): return lax.ppermute(x, 'yl', [(0, 1), (1, 0)])  10.8 us
  transfers between devices with their start and end apart: 19, of which 10 were waited for; matrix products, arithmetic and copies ran while one was open for 5% of the time, Pallas kernels for 8%

profile of v3, /device:TPU:6, one launch (start us, length us, event | category | flops | bytes accessed | tf_op | source)
XLA Modules:
  0.0 260.6 jit_solution(3975154624785484161)
XLA Ops:
  7.2 2.8 %dynamic-slice_bitcast_fusion.2 = bf16[112,7168]{1,0:T(8,128)(2,1)} fusion(bf16[1,224,7168]{2,1,0:T(8,128)(2,1)} %param.8, s32[]{:T(128)S(6)} %select_n.25), kind=kLoop, calls=%fused_computation.2 | loop fusion | bytes 3211268 | tf_op jit(solution)/shard_map/dynamic_slice | solution.py:268
  16.3 4.7 %row_slots.1 = bf16[8,8,2,16,896]{4,3,2,1,0:T(8,128)(2,1)} custom-call(s32[8]{0:T(128)S(1)} %stack.86.tab, bf16[224,7168]{1,0:T(8,128)(2,1)S(1)} %bitcast.43, bf16[112,7168]{1,0:T(8,128)(2,1)} %collective-permute-done.theirs), custom_call_target="tpu_custom_call" | custom-call | flops 5000000 | bytes 10000000 | tf_op jit(solution)/shard_map/row_slots/pallas_call | solution.py:75
  21.0 2.7 %column_blocks.1 = bf16[8,224,896]{2,1,0:T(8,128)(2,1)S(1)} custom-call(bf16[224,7168]{1,0:T(8,128)(2,1)} %bitcast.42), custom_call_target="tpu_custom_call" | custom-call | flops 1000000 | bytes 6400000 | tf_op jit(solution)/shard_map/column_blocks/pallas_call | solution.py:101
  25.5 7.7 %all-to-all-start = ((bf16[8,224,896]{2,1,0:T(8,128)(2,1)}), bf16[8,224,896]{2,1,0:T(8,128)(2,1)}, u32[]{:S(2)}, u32[]{:S(2)}) async-start(bf16[8,224,896]{2,1,0:T(8,128)(2,1)} %copy-done.3), calls=%async_computation.1 | async-start | bytes 6422528 | tf_op jit(solution)/shard_map/all_to_all | solution.py:327
  36.8 4.5 %slots.1 = bf16[8,2,112,896]{3,2,1,0:T(8,128)(2,1)} custom-call(s32[8]{0:T(128)S(1)} %stack.86.tab, bf16[224,7168]{1,0:T(8,128)(2,1)} %bitcast.40, bf16[112,7168]{1,0:T(8,128)(2,1)S(1)} %collective-permute-done.1.theirs), custom_call_target="tpu_custom_call" | custom-call | flops 5000000 | bytes 10000000 | tf_op jit(solution)/shard_map/slots/pallas_call | solution.py:40
  41.4 39.6 %all-to-all-done.own = bf16[8,224,896]{2,1,0:T(8,128)(2,1)} async-done(((bf16[8,224,896]{2,1,0:T(8,128)(2,1)}), bf16[8,224,896]{2,1,0:T(8,128)(2,1)}, u32[]{:S(2)}, u32[]{:S(2)}) %all-to-all-start) | async-done | bytes 3211296 | tf_op jit(solution)/shard_map/all_to_all | solution.py:327
  82.1 19.7 %all_to_all.20 = bf16[16,2,16,896]{3,2,1,0:T(8,128)(2,1)S(1)} all-to-all(bf16[16,2,16,896]{3,2,1,0:T(8,128)(2,1)S(1)} %bitcast.45), channel_id=1, replica_groups=mesh['z'=8,'yl'=2,'c'=2,'yh'=2,'x'=4] {'yl','yh','x'}, dimensions={0} | all-to-all | bytes 1835008 | tf_op jit(solution)/shard_map/all_to_all | solution.py:335
  103.3 6.7 %all-to-all-start.2 = ((bf16[8,224,512]{2,1,0:T(8,128)(2,1)}), bf16[8,224,512]{2,1,0:T(8,128)(2,1)}, u32[]{:S(2)}, u32[]{:S(2)}) async-start(bf16[8,224,512]{2,1,0:T(8,128)(2,1)} %broadcast_in_dim.33), calls=%async_computation.4 | async-start | bytes 3670016 | tf_op jit(solution)/shard_map/all_to_all | solution.py:339
  110.0 5.9 %collective-permute-start.4 = (bf16[8,2,16,896]{3,2,1,0:T(8,128)(2,1)S(1)}, bf16[8,2,16,896]{3,2,1,0:T(8,128)(2,1)S(1)}, u32[]{:S(2)}, u32[]{:S(2)}) collective-permute-start(bf16[8,2,16,896]{3,2,1,0:T(8,128)(2,1)S(1)} %slice_add_fusion.refs_0_), channel_id=1, source_target_pairs={{0,224},{32,0},{64,32},{96,64},{128,96},{160,128},{192,160},{224,1... | collective-permute-start | bytes 1376264 | tf_op jit(solution)/shard_map/ppermute | solution.py:285
  115.9 19.4 %collective-permute-done.4.refs_2_ = bf16[8,2,16,896]{3,2,1,0:T(8,128)(2,1)S(1)} collective-permute-done((bf16[8,2,16,896]{3,2,1,0:T(8,128)(2,1)S(1)}, bf16[8,2,16,896]{3,2,1,0:T(8,128)(2,1)S(1)}, u32[]{:S(2)}, u32[]{:S(2)}) %collective-permute-start.4) | collective-permute-done | bytes 458784 | tf_op jit(solution)/shard_map/ppermute | solution.py:285
  135.3 3.7 %collective-permute-start.5 = (bf16[8,2,16,896]{3,2,1,0:T(8,128)(2,1)S(1)}, bf16[8,2,16,896]{3,2,1,0:T(8,128)(2,1)S(1)}, u32[]{:S(2)}, u32[]{:S(2)}) collective-permute-start(bf16[8,2,16,896]{3,2,1,0:T(8,128)(2,1)S(1)} %collective-permute-done.4.refs_2_), channel_id=1, source_target_pairs={{0,224},{32,0},{64,32},{96,64},{128,96},{160,128},{192,160},{224,1... | collective-permute-start | bytes 1376264 | tf_op jit(solution)/shard_map/ppermute | solution.py:285
  140.4 6.4 %collective-permute-done.5.refs_4_ = bf16[8,2,16,896]{3,2,1,0:T(8,128)(2,1)S(1)} collective-permute-done((bf16[8,2,16,896]{3,2,1,0:T(8,128)(2,1)S(1)}, bf16[8,2,16,896]{3,2,1,0:T(8,128)(2,1)S(1)}, u32[]{:S(2)}, u32[]{:S(2)}) %collective-permute-start.5) | collective-permute-done | bytes 458784 | tf_op jit(solution)/shard_map/ppermute | solution.py:285
  146.9 2.8 %collective-permute-done.3.refs_3_ = bf16[8,2,16,896]{3,2,1,0:T(8,128)(2,1)S(1)} collective-permute-done((bf16[8,2,16,896]{3,2,1,0:T(8,128)(2,1)S(1)}, bf16[8,2,16,896]{3,2,1,0:T(8,128)(2,1)S(1)}, u32[]{:S(2)}, u32[]{:S(2)}) %collective-permute-start.3) | collective-permute-done | bytes 458784 | tf_op jit(solution)/shard_map/ppermute | solution.py:285
  149.7 3.2 %collective-permute-start.8 = (bf16[8,2,16,896]{3,2,1,0:T(8,128)(2,1)S(1)}, bf16[8,2,16,896]{3,2,1,0:T(8,128)(2,1)S(1)}, u32[]{:S(2)}, u32[]{:S(2)}) collective-permute-start(bf16[8,2,16,896]{3,2,1,0:T(8,128)(2,1)S(1)} %collective-permute-done.5.refs_4_), channel_id=1, source_target_pairs={{0,224},{32,0},{64,32},{96,64},{128,96},{160,128},{192,160},{224,1... | collective-permute-start | bytes 1376264 | tf_op jit(solution)/shard_map/ppermute | solution.py:285
  155.8 4.1 %collective-permute-done.7.refs_5_ = bf16[8,2,16,896]{3,2,1,0:T(8,128)(2,1)S(1)} collective-permute-done((bf16[8,2,16,896]{3,2,1,0:T(8,128)(2,1)S(1)}, bf16[8,2,16,896]{3,2,1,0:T(8,128)(2,1)S(1)}, u32[]{:S(2)}, u32[]{:S(2)}) %collective-permute-start.7) | collective-permute-done | bytes 458784 | tf_op jit(solution)/shard_map/ppermute | solution.py:285
  160.4 2.9 %collective-permute-start.10 = (bf16[4,2,16,896]{3,2,1,0:T(8,128)(2,1)S(1)}, bf16[4,2,16,896]{3,2,1,0:T(8,128)(2,1)S(1)}, u32[]{:S(2)}, u32[]{:S(2)}) collective-permute-start(bf16[4,2,16,896]{3,2,1,0:T(8,128)(2,1)S(1)} %slice.27), channel_id=1, source_target_pairs={{0,224},{32,0},{64,32},{96,64},{128,96},{160,128},{192,160},{224,1... | collective-permute-start | bytes 688136 | tf_op jit(solution)/shard_map/ppermute | solution.py:290
  164.7 2.4 collective-permute-done.9
  168.8 10.8 %collective-permute-done.6 = bf16[1,2,112,896]{3,2,1,0:T(8,128)(2,1)S(1)} collective-permute-done((bf16[1,2,112,896]{3,2,1,0:T(8,128)(2,1)S(1)}, bf16[1,2,112,896]{3,2,1,0:T(8,128)(2,1)S(1)}, u32[]{:S(2)}, u32[]{:S(2)}) %collective-permute-start.6) | collective-permute-done | bytes 401440 | tf_op jit(solution)/shard_map/ppermute | solution.py:263
  182.8 13.8 %step.1 = (bf16[512,896]{1,0:T(8,128)(2,1)}, bf16[8,224,896]{2,1,0:T(8,128)(2,1)}) custom-call(s32[8]{0:T(128)S(1)} %stack.86.tab, f32[1]{0:T(128)} %bitcast.12.rate, bf16[8,224,512]{2,1,0:T(8,128)(2,1)} %all-to-all-done.2.tokens, bf16[8,224,896]{2,1,0:T(8,128)(2,1)} %all-to-all-done.own, bf16[512,896]{1,0:T(8,128)(2,1)S(1)} %bitcast.44, ...), custom_call_target="tpu_custom_call" | custom-call | flops 3288334336 | bytes 20000000 | tf_op jit(solution)/shard_map/step/pallas_call | solution.py:224
  196.6 7.2 %all-to-all-start.3 = ((bf16[8,224,896]{2,1,0:T(8,128)(2,1)}), bf16[8,224,896]{2,1,0:T(8,128)(2,1)}, u32[]{:S(2)}, u32[]{:S(2)}) async-start(bf16[8,224,896]{2,1,0:T(8,128)(2,1)} %get-tuple-element.29), calls=%async_computation.5 | async-start | bytes 6422528 | tf_op jit(solution)/shard_map/all_to_all | solution.py:352
  203.8 22.3 %all-gather.2.cloned.1.call-done.gathered = bf16[8,2,112,896]{3,2,1,0:T(8,128)(2,1)} async-done(((bf16[1,2,112,896]{3,2,1,0:T(8,128)(2,1)}), bf16[8,2,112,896]{3,2,1,0:T(8,128)(2,1)}) %all-gather.2.cloned.1.call-update) | async-done | bytes 3211280 | tf_op jit(solution)/shard_map/all_gather | solution.py:276
  226.1 2.8 %dynamic-slice_bitcast_fusion = bf16[8,112,896]{2,1,0:T(8,128)(2,1)} fusion(bf16[8,2,112,896]{3,2,1,0:T(8,128)(2,1)} %all-gather.2.cloned.1.call-done.gathered, s32[]{:T(128)S(6)} %select_n.28), kind=kLoop, calls=%fused_computation | loop fusion | bytes 3211268 | tf_op jit(solution)/shard_map/jit(dynamic_index_in_dim)/squeeze | solution.py:353
  228.9 18.4 %all-to-all-done.3.back = bf16[8,224,896]{2,1,0:T(8,128)(2,1)} async-done(((bf16[8,224,896]{2,1,0:T(8,128)(2,1)}), bf16[8,224,896]{2,1,0:T(8,128)(2,1)}, u32[]{:S(2)}, u32[]{:S(2)}) %all-to-all-start.3) | async-done | bytes 3211296 | tf_op jit(solution)/shard_map/all_to_all | solution.py:352
  247.4 6.7 %final.1 = bf16[224,7168]{1,0:T(8,128)(2,1)} custom-call(s32[8]{0:T(128)S(1)} %stack.86.tab, f32[1]{0:T(128)} %bitcast.12.rate, bf16[224,7168]{1,0:T(8,128)(2,1)S(1)} %bitcast.41, bf16[8,2,112,896]{3,2,1,0:T(8,128)(2,1)} %all-gather.2.cloned.1.call-done.gathered, bf16[8,112,896]{2,1,0:T(8,128)(2,1)} %collective-permute-done.12.received, ...), custom_call_target="tpu_custom_call" | custom-call | flops 5000000 | bytes 13000000 | tf_op jit(solution)/shard_map/final/pallas_call | solution.py:138
  (73 shorter events, 20.6 us)
Async XLA Ops:
  7.2 9.1 %copy-start.2 = (bf16[1,224,7168]{2,1,0:T(8,128)(2,1)S(1)}, bf16[1,224,7168]{2,1,0:T(8,128)(2,1)}, u32[]{:S(2)}) copy-start(bf16[1,224,7168]{2,1,0:T(8,128)(2,1)} %param.8) | copy-start | bytes 9633796
  7.2 73.8 %reduce-scatter.3.cloned.1.call-start = ((), (), s32[]{:S(2)}) async-start(), calls=%async_computation.6 | async-start | bytes 4128768 | tf_op jit(solution)/shard_map/reduce_scatter | solution.py:272
  10.1 6.2 %collective-permute-start = (bf16[112,7168]{1,0:T(8,128)(2,1)}, bf16[112,7168]{1,0:T(8,128)(2,1)}, u32[]{:S(2)}, u32[]{:S(2)}) collective-permute-start(bf16[112,7168]{1,0:T(8,128)(2,1)} %dynamic-slice_bitcast_fusion.2), channel_id=1, source_target_pairs={{0,8},{8,0},{1,9},{9,1},{2,10},{10,2},{3,11},{11,3},{4,12},{12,4},... | collective-permute-start | bytes 4816904 | tf_op jit(solution)/shard_map/ppermute | solution.py:259
  25.5 55.6 %all-to-all-start = ((bf16[8,224,896]{2,1,0:T(8,128)(2,1)}), bf16[8,224,896]{2,1,0:T(8,128)(2,1)}, u32[]{:S(2)}, u32[]{:S(2)}) async-start(bf16[8,224,896]{2,1,0:T(8,128)(2,1)} %copy-done.3), calls=%async_computation.1 | async-start | bytes 6422528 | tf_op jit(solution)/shard_map/all_to_all | solution.py:327
  33.1 116.5 %reduce-scatter.5.cloned.1.call-start = ((), (), s32[]{:S(2)}) async-start(), calls=%async_computation.7 | async-start | bytes 3612672 | tf_op jit(solution)/shard_map/reduce_scatter | solution.py:272
  33.3 3.5 %collective-permute-start.1 = (bf16[112,7168]{1,0:T(8,128)(2,1)S(1)}, bf16[112,7168]{1,0:T(8,128)(2,1)S(1)}, u32[]{:S(2)}, u32[]{:S(2)}) collective-permute-start(bf16[112,7168]{1,0:T(8,128)(2,1)S(1)} %dynamic-slice_bitcast_fusion.1), channel_id=1, source_target_pairs={{0,8},{8,0},{1,9},{9,1},{2,10},{10,2},{3,11},{11,3},{4,12},{12,4},... | collective-permute-start | bytes 4816904 | tf_op jit(solution)/shard_map/ppermute | solution.py:259
  82.1 19.8 %copy-start.9 = (bf16[1,512,224]{1,2,0:T(8,128)(2,1)S(1)}, bf16[1,512,224]{1,2,0:T(8,128)(2,1)}, u32[]{:S(2)}) copy-start(bf16[1,512,224]{1,2,0:T(8,128)(2,1)} %param.7) | copy-start | bytes 688132
  103.3 46.3 %all-to-all-start.2 = ((bf16[8,224,512]{2,1,0:T(8,128)(2,1)}), bf16[8,224,512]{2,1,0:T(8,128)(2,1)}, u32[]{:S(2)}, u32[]{:S(2)}) async-start(bf16[8,224,512]{2,1,0:T(8,128)(2,1)} %broadcast_in_dim.33), calls=%async_computation.4 | async-start | bytes 3670016 | tf_op jit(solution)/shard_map/all_to_all | solution.py:339
  110.0 116.1 %all-gather.2.cloned.1.call-start = ((), (), s32[]{:S(2)}) async-start(), calls=%async_computation.8 | async-start | bytes 3612672 | tf_op jit(solution)/shard_map/all_gather | solution.py:276
  110.0 25.3 %collective-permute-start.4 = (bf16[8,2,16,896]{3,2,1,0:T(8,128)(2,1)S(1)}, bf16[8,2,16,896]{3,2,1,0:T(8,128)(2,1)S(1)}, u32[]{:S(2)}, u32[]{:S(2)}) collective-permute-start(bf16[8,2,16,896]{3,2,1,0:T(8,128)(2,1)S(1)} %slice_add_fusion.refs_0_), channel_id=1, source_target_pairs={{0,224},{32,0},{64,32},{96,64},{128,96},{160,128},{192,160},{224,1... | collective-permute-start | bytes 1376264 | tf_op jit(solution)/shard_map/ppermute | solution.py:285
  115.9 23.1 %collective-permute-start.2 = (bf16[8,2,16,896]{3,2,1,0:T(8,128)(2,1)S(1)}, bf16[8,2,16,896]{3,2,1,0:T(8,128)(2,1)S(1)}, u32[]{:S(2)}, u32[]{:S(2)}) collective-permute-start(bf16[8,2,16,896]{3,2,1,0:T(8,128)(2,1)S(1)} %slice_add_fusion.refs_0_), channel_id=1, source_target_pairs={{0,32},{32,64},{64,96},{96,128},{128,160},{160,192},{192,224},{224... | collective-permute-start | bytes 1376264 | tf_op jit(solution)/shard_map/ppermute | solution.py:285
  135.3 11.5 %collective-permute-start.5 = (bf16[8,2,16,896]{3,2,1,0:T(8,128)(2,1)S(1)}, bf16[8,2,16,896]{3,2,1,0:T(8,128)(2,1)S(1)}, u32[]{:S(2)}, u32[]{:S(2)}) collective-permute-start(bf16[8,2,16,896]{3,2,1,0:T(8,128)(2,1)S(1)} %collective-permute-done.4.refs_2_), channel_id=1, source_target_pairs={{0,224},{32,0},{64,32},{96,64},{128,96},{160,128},{192,160},{224,1... | collective-permute-start | bytes 1376264 | tf_op jit(solution)/shard_map/ppermute | solution.py:285
  139.0 10.6 %collective-permute-start.3 = (bf16[8,2,16,896]{3,2,1,0:T(8,128)(2,1)S(1)}, bf16[8,2,16,896]{3,2,1,0:T(8,128)(2,1)S(1)}, u32[]{:S(2)}, u32[]{:S(2)}) collective-permute-start(bf16[8,2,16,896]{3,2,1,0:T(8,128)(2,1)S(1)} %collective-permute-done.2.refs_1_), channel_id=1, source_target_pairs={{0,32},{32,64},{64,96},{96,128},{128,160},{160,192},{192,224},{224... | collective-permute-start | bytes 1376264 | tf_op jit(solution)/shard_map/ppermute | solution.py:285
  149.6 15.1 %copy-start.4 = (bf16[8,2,16,896]{3,2,1,0:T(8,128)(2,1)}, bf16[8,2,16,896]{3,2,1,0:T(8,128)(2,1)S(1)}, u32[]{:S(2)}) copy-start(bf16[8,2,16,896]{3,2,1,0:T(8,128)(2,1)S(1)} %collective-permute-done.3.refs_3_) | copy-start | bytes 1376260
  149.6 10.2 %collective-permute-start.7 = (bf16[8,2,16,896]{3,2,1,0:T(8,128)(2,1)S(1)}, bf16[8,2,16,896]{3,2,1,0:T(8,128)(2,1)S(1)}, u32[]{:S(2)}, u32[]{:S(2)}) collective-permute-start(bf16[8,2,16,896]{3,2,1,0:T(8,128)(2,1)S(1)} %collective-permute-done.3.refs_3_), channel_id=1, source_target_pairs={{0,32},{32,64},{64,96},{96,128},{128,160},{160,192},{192,224},{224... | collective-permute-start | bytes 1376264 | tf_op jit(solution)/shard_map/ppermute | solution.py:285
  149.7 10.7 %collective-permute-start.8 = (bf16[8,2,16,896]{3,2,1,0:T(8,128)(2,1)S(1)}, bf16[8,2,16,896]{3,2,1,0:T(8,128)(2,1)S(1)}, u32[]{:S(2)}, u32[]{:S(2)}) collective-permute-start(bf16[8,2,16,896]{3,2,1,0:T(8,128)(2,1)S(1)} %collective-permute-done.5.refs_4_), channel_id=1, source_target_pairs={{0,224},{32,0},{64,32},{96,64},{128,96},{160,128},{192,160},{224,1... | collective-permute-start | bytes 1376264 | tf_op jit(solution)/shard_map/ppermute | solution.py:285
  155.0 12.9 %copy-start.8 = (bf16[1,2,112,896]{3,2,1,0:T(8,128)(2,1)S(1)}, bf16[1,2,112,896]{3,2,1,0:T(8,128)(2,1)}, u32[]{:S(2)}) copy-start(bf16[1,2,112,896]{3,2,1,0:T(8,128)(2,1)} %reduce-scatter.5.cloned.1.call-done) | copy-start | bytes 1204228
  159.8 7.3 %collective-permute-start.9 = (bf16[4,2,16,896]{3,2,1,0:T(8,128)(2,1)S(1)}, bf16[4,2,16,896]{3,2,1,0:T(8,128)(2,1)S(1)}, u32[]{:S(2)}, u32[]{:S(2)}) collective-permute-start(bf16[4,2,16,896]{3,2,1,0:T(8,128)(2,1)S(1)} %slice.26), channel_id=1, source_target_pairs={{0,32},{32,64},{64,96},{96,128},{128,160},{160,192},{192,224},{224... | collective-permute-start | bytes 688136 | tf_op jit(solution)/shard_map/ppermute | solution.py:290
  160.4 6.8 %collective-permute-start.10 = (bf16[4,2,16,896]{3,2,1,0:T(8,128)(2,1)S(1)}, bf16[4,2,16,896]{3,2,1,0:T(8,128)(2,1)S(1)}, u32[]{:S(2)}, u32[]{:S(2)}) collective-permute-start(bf16[4,2,16,896]{3,2,1,0:T(8,128)(2,1)S(1)} %slice.27), channel_id=1, source_target_pairs={{0,224},{32,0},{64,32},{96,64},{128,96},{160,128},{192,160},{224,1... | collective-permute-start | bytes 688136 | tf_op jit(solution)/shard_map/ppermute | solution.py:290
  167.9 11.7 %collective-permute-start.11 = (bf16[8,8,16,896]{3,2,1,0:T(8,128)(2,1)}, bf16[8,8,16,896]{3,2,1,0:T(8,128)(2,1)}, u32[]{:S(2)}, u32[]{:S(2)}) collective-permute-start(bf16[8,8,16,896]{3,2,1,0:T(8,128)(2,1)} %bitcast_dynamic-update-slice_fusion), channel_id=1, source_target_pairs={{0,8},{8,0},{1,9},{9,1},{2,10},{10,2},{3,11},{11,3},{4,12},{12,4},... | collective-permute-start | bytes 5505032 | tf_op jit(solution)/shard_map/ppermute | solution.py:259
  167.9 11.7 %collective-permute-start.6 = (bf16[1,2,112,896]{3,2,1,0:T(8,128)(2,1)S(1)}, bf16[1,2,112,896]{3,2,1,0:T(8,128)(2,1)S(1)}, u32[]{:S(2)}, u32[]{:S(2)}) collective-permute-start(bf16[1,2,112,896]{3,2,1,0:T(8,128)(2,1)S(1)} %copy-done.8), channel_id=1, source_target_pairs={{0,16},{16,0},{1,17},{17,1},{2,18},{18,2},{3,19},{19,3},{4,20},{20... | collective-permute-start | bytes 1204232 | tf_op jit(solution)/shard_map/ppermute | solution.py:263
  196.6 50.8 %all-to-all-start.3 = ((bf16[8,224,896]{2,1,0:T(8,128)(2,1)}), bf16[8,224,896]{2,1,0:T(8,128)(2,1)}, u32[]{:S(2)}, u32[]{:S(2)}) async-start(bf16[8,224,896]{2,1,0:T(8,128)(2,1)} %get-tuple-element.29), calls=%async_computation.5 | async-start | bytes 6422528 | tf_op jit(solution)/shard_map/all_to_all | solution.py:352
  203.8 43.6 %copy-start.1 = (bf16[1,224,7168]{2,1,0:T(8,128)(2,1)S(1)}, bf16[1,224,7168]{2,1,0:T(8,128)(2,1)}, u32[]{:S(2)}) copy-start(bf16[1,224,7168]{2,1,0:T(8,128)(2,1)} %param.9) | copy-start | bytes 9633796
  228.9 18.4 %collective-permute-start.12 = (bf16[8,112,896]{2,1,0:T(8,128)(2,1)}, bf16[8,112,896]{2,1,0:T(8,128)(2,1)}, u32[]{:S(2)}, u32[]{:S(2)}) collective-permute-start(bf16[8,112,896]{2,1,0:T(8,128)(2,1)} %dynamic-slice_bitcast_fusion), channel_id=1, source_target_pairs={{0,8},{8,0},{1,9},{9,1},{2,10},{10,2},{3,11},{11,3},{4,12},{12,4},... | collective-permute-start | bytes 4816904 | tf_op jit(solution)/shard_map/ppermute | solution.py:259
  (8 other events, 17.5 us)
Sparse Core Ops, SparseCore 0:
  21.1 53.4 reduce-scatter.2
  81.2 58.8 reduce-scatter.4
  180.7 45.3 all-gather.1

commit v4 on v3

--- a/solution.py
+++ b/solution.py
@@ -341,12 +341,12 @@
     )
     pieces, (m_mine, all_tokens) = ring(w_mine, (m_mine, all_tokens))
     m_across = swap_column(m_mine)
+    pieces[-1], m_across = lax.optimization_barrier((pieces[-1], m_across))
     w_other = swap_core(
         jnp.stack(
             [lax.dynamic_index_in_dim(p, partner_slot, axis=1, keepdims=False) for p in pieces]
         )
     )
-    m_across, w_other = lax.optimization_barrier((m_across, w_other))
     m_won = gather(m_mine + m_across)
     activation, back = step(tab, rate, all_tokens, own_columns, cotangent[0], w_other, pieces)
     back = lax.all_to_all(back, TP, 0, 0, tiled=True)

time: 263 us -> 263 us (level)
  waiting for transfers between devices: 127 us -> 131 us
    all_to_all x1, waiting for transfers between devices: 18.4 us -> 31 us  [local(): back = lax.all_to_all(back, TP, 0, 0, tiled=True)]
    ppermute x1, waiting for transfers between devices: 10.8 us -> 0.01 us  [swap_column(): return lax.ppermute(x, 'yl', [(0, 1), (1, 0)])]
    all_gather x1, waiting for transfers between devices: 22.3 us -> 12.2 us  [gather(): return lax.all_gather(mine, 'z', axis=0, tiled=True)]
    ppermute x4, waiting for transfers between devices: 1.14 us -> 4.98 us  [swap_core(): return lax.ppermute(x, 'c', [(0, 1), (1, 0)])]
    ppermute x1, waiting for transfers between devices: 0.01 us -> 3.42 us  [ring(): lax.ppermute(high[half:], 'z', down)]
    ppermute x6, waiting for transfers between devices: 32.7 us -> 35.6 us  [ring(): low, high = (lax.ppermute(low, 'z', up), lax.ppermute(high, 'z', down))]
    unnamed x34 -> x63, local copies, waits for them, and re-layouts: 10.2 us -> 9.53 us
  transfers between devices with their start and end apart: 19 -> 19, of which waited for: 10 -> 10; matrix products, arithmetic and copies ran while one was open for 5% -> 3% of each run, Pallas kernels for 8% -> 8%
where the time goes in v4:
time: 263 us; the launch traced here: 261 us
  waiting for transfers between devices  131 us (50%)
  starting transfers between devices  38.1 us (14%)
  Pallas kernels  32.5 us (12%)
  blocking collectives  19.7 us (7%)
  between operations  18.6 us (7%)
  local copies, waits for them, and re-layouts  16.9 us (6%)
  other arithmetic  4.93 us (2%)
    all_to_all x1, waiting for transfers between devices, local(): own_columns = lax.all_to_all(column_blocks(w), TP, 0, 0, tiled=True)  39.5 us
    ppermute x6, waiting for transfers between devices, ring(): low, high = (lax.ppermute(low, 'z', up), lax.ppermute(high, 'z', down))  35.6 us
    all_to_all x1, waiting for transfers between devices, local(): back = lax.all_to_all(back, TP, 0, 0, tiled=True)  31 us
    all_to_all x1, blocking collectives, local(): both = lax.all_to_all(both, ('yl',) + TP, 0, 0, tiled=True)  19.7 us
    pallas_call x1, Pallas kernels, step(): pl.pallas_call(step_kernel, grid_spec=pltpu.PrefetchScalarGridSpec(num_sc...  13.8 us
    all_gather x1, waiting for transfers between devices, gather(): return lax.all_gather(mine, 'z', axis=0, tiled=True)  12.2 us
    ppermute x6, starting transfers between devices, ring(): low, high = (lax.ppermute(low, 'z', up), lax.ppermute(high, 'z', down))  11.3 us
    unnamed x63, local copies, waits for them, and re-layouts  9.53 us
  transfers between devices with their start and end apart: 19, of which 10 were waited for; matrix products, arithmetic and copies ran while one was open for 3% of the time, Pallas kernels for 8%

profile of v4, /device:TPU:6, one launch (start us, length us, event | category | flops | bytes accessed | tf_op | source)
XLA Modules:
  0.0 261.2 jit_solution(4758489239148331302)
XLA Ops:
  7.2 2.8 %dynamic-slice_bitcast_fusion.2 = bf16[112,7168]{1,0:T(8,128)(2,1)} fusion(bf16[1,224,7168]{2,1,0:T(8,128)(2,1)} %param.8, s32[]{:T(128)S(6)} %select_n.25), kind=kLoop, calls=%fused_computation.2 | loop fusion | bytes 3211268 | tf_op jit(solution)/shard_map/dynamic_slice | solution.py:268
  16.1 4.7 %row_slots.1 = bf16[8,8,2,16,896]{4,3,2,1,0:T(8,128)(2,1)} custom-call(s32[8]{0:T(128)S(1)} %stack.86.tab, bf16[224,7168]{1,0:T(8,128)(2,1)S(1)} %bitcast.43, bf16[112,7168]{1,0:T(8,128)(2,1)} %collective-permute-done.theirs), custom_call_target="tpu_custom_call" | custom-call | flops 5000000 | bytes 10000000 | tf_op jit(solution)/shard_map/row_slots/pallas_call | solution.py:75
  20.9 2.7 %column_blocks.1 = bf16[8,224,896]{2,1,0:T(8,128)(2,1)S(1)} custom-call(bf16[224,7168]{1,0:T(8,128)(2,1)} %bitcast.42), custom_call_target="tpu_custom_call" | custom-call | flops 1000000 | bytes 6400000 | tf_op jit(solution)/shard_map/column_blocks/pallas_call | solution.py:101
  25.3 7.7 %all-to-all-start = ((bf16[8,224,896]{2,1,0:T(8,128)(2,1)}), bf16[8,224,896]{2,1,0:T(8,128)(2,1)}, u32[]{:S(2)}, u32[]{:S(2)}) async-start(bf16[8,224,896]{2,1,0:T(8,128)(2,1)} %copy-done.3), calls=%async_computation.1 | async-start | bytes 6422528 | tf_op jit(solution)/shard_map/all_to_all | solution.py:327
  36.7 4.7 %slots.1 = bf16[8,2,112,896]{3,2,1,0:T(8,128)(2,1)} custom-call(s32[8]{0:T(128)S(1)} %stack.86.tab, bf16[224,7168]{1,0:T(8,128)(2,1)} %bitcast.40, bf16[112,7168]{1,0:T(8,128)(2,1)S(1)} %collective-permute-done.1.theirs), custom_call_target="tpu_custom_call" | custom-call | flops 5000000 | bytes 10000000 | tf_op jit(solution)/shard_map/slots/pallas_call | solution.py:40
  41.4 39.5 %all-to-all-done.own = bf16[8,224,896]{2,1,0:T(8,128)(2,1)} async-done(((bf16[8,224,896]{2,1,0:T(8,128)(2,1)}), bf16[8,224,896]{2,1,0:T(8,128)(2,1)}, u32[]{:S(2)}, u32[]{:S(2)}) %all-to-all-start) | async-done | bytes 3211296 | tf_op jit(solution)/shard_map/all_to_all | solution.py:327
  82.0 19.7 %all_to_all.20 = bf16[16,2,16,896]{3,2,1,0:T(8,128)(2,1)S(1)} all-to-all(bf16[16,2,16,896]{3,2,1,0:T(8,128)(2,1)S(1)} %bitcast.45), channel_id=1, replica_groups=mesh['z'=8,'yl'=2,'c'=2,'yh'=2,'x'=4] {'yl','yh','x'}, dimensions={0} | all-to-all | bytes 1835008 | tf_op jit(solution)/shard_map/all_to_all | solution.py:335
  103.2 6.7 %all-to-all-start.2 = ((bf16[8,224,512]{2,1,0:T(8,128)(2,1)}), bf16[8,224,512]{2,1,0:T(8,128)(2,1)}, u32[]{:S(2)}, u32[]{:S(2)}) async-start(bf16[8,224,512]{2,1,0:T(8,128)(2,1)} %broadcast_in_dim.33), calls=%async_computation.4 | async-start | bytes 3670016 | tf_op jit(solution)/shard_map/all_to_all | solution.py:339
  109.9 1.9 collective-permute-start.2
  111.8 4.0 %collective-permute-start.4 = (bf16[8,2,16,896]{3,2,1,0:T(8,128)(2,1)S(1)}, bf16[8,2,16,896]{3,2,1,0:T(8,128)(2,1)S(1)}, u32[]{:S(2)}, u32[]{:S(2)}) collective-permute-start(bf16[8,2,16,896]{3,2,1,0:T(8,128)(2,1)S(1)} %slice_add_fusion.refs_0_), channel_id=1, source_target_pairs={{0,224},{32,0},{64,32},{96,64},{128,96},{160,128},{192,160},{224,1... | collective-permute-start | bytes 1376264 | tf_op jit(solution)/shard_map/ppermute | solution.py:285
  115.8 20.1 %collective-permute-done.2.refs_1_ = bf16[8,2,16,896]{3,2,1,0:T(8,128)(2,1)S(1)} collective-permute-done((bf16[8,2,16,896]{3,2,1,0:T(8,128)(2,1)S(1)}, bf16[8,2,16,896]{3,2,1,0:T(8,128)(2,1)S(1)}, u32[]{:S(2)}, u32[]{:S(2)}) %collective-permute-start.2) | collective-permute-done | bytes 458784 | tf_op jit(solution)/shard_map/ppermute | solution.py:285
  136.0 3.2 %collective-permute-start.5 = (bf16[8,2,16,896]{3,2,1,0:T(8,128)(2,1)S(1)}, bf16[8,2,16,896]{3,2,1,0:T(8,128)(2,1)S(1)}, u32[]{:S(2)}, u32[]{:S(2)}) collective-permute-start(bf16[8,2,16,896]{3,2,1,0:T(8,128)(2,1)S(1)} %collective-permute-done.4.refs_2_), channel_id=1, source_target_pairs={{0,224},{32,0},{64,32},{96,64},{128,96},{160,128},{192,160},{224,1... | collective-permute-start | bytes 1376264 | tf_op jit(solution)/shard_map/ppermute | solution.py:285
  139.2 8.9 %collective-permute-done.3.refs_3_ = bf16[8,2,16,896]{3,2,1,0:T(8,128)(2,1)S(1)} collective-permute-done((bf16[8,2,16,896]{3,2,1,0:T(8,128)(2,1)S(1)}, bf16[8,2,16,896]{3,2,1,0:T(8,128)(2,1)S(1)}, u32[]{:S(2)}, u32[]{:S(2)}) %collective-permute-start.3) | collective-permute-done | bytes 458784 | tf_op jit(solution)/shard_map/ppermute | solution.py:285
  151.7 6.6 %collective-permute-done.7.refs_6_ = bf16[8,2,16,896]{3,2,1,0:T(8,128)(2,1)S(1)} collective-permute-done((bf16[8,2,16,896]{3,2,1,0:T(8,128)(2,1)S(1)}, bf16[8,2,16,896]{3,2,1,0:T(8,128)(2,1)S(1)}, u32[]{:S(2)}, u32[]{:S(2)}) %collective-permute-start.7) | collective-permute-done | bytes 458784 | tf_op jit(solution)/shard_map/ppermute | solution.py:285
  158.3 3.1 %collective-permute-start.9 = (bf16[4,2,16,896]{3,2,1,0:T(8,128)(2,1)S(1)}, bf16[4,2,16,896]{3,2,1,0:T(8,128)(2,1)S(1)}, u32[]{:S(2)}, u32[]{:S(2)}) collective-permute-start(bf16[4,2,16,896]{3,2,1,0:T(8,128)(2,1)S(1)} %slice.27), channel_id=1, source_target_pairs={{0,224},{32,0},{64,32},{96,64},{128,96},{160,128},{192,160},{224,1... | collective-permute-start | bytes 688136 | tf_op jit(solution)/shard_map/ppermute | solution.py:290
  161.6 3.4 %collective-permute-done.9 = bf16[4,2,16,896]{3,2,1,0:T(8,128)(2,1)S(1)} collective-permute-done((bf16[4,2,16,896]{3,2,1,0:T(8,128)(2,1)S(1)}, bf16[4,2,16,896]{3,2,1,0:T(8,128)(2,1)S(1)}, u32[]{:S(2)}, u32[]{:S(2)}) %collective-permute-start.9) | collective-permute-done | bytes 229408 | tf_op jit(solution)/shard_map/ppermute | solution.py:290
  165.0 3.8 %collective-permute-done.8 = bf16[4,2,16,896]{3,2,1,0:T(8,128)(2,1)S(1)} collective-permute-done((bf16[4,2,16,896]{3,2,1,0:T(8,128)(2,1)S(1)}, bf16[4,2,16,896]{3,2,1,0:T(8,128)(2,1)S(1)}, u32[]{:S(2)}, u32[]{:S(2)}) %collective-permute-start.8) | collective-permute-done | bytes 229408 | tf_op jit(solution)/shard_map/ppermute | solution.py:290
  171.9 3.8 %collective-permute-done.11.received = bf16[8,8,16,896]{3,2,1,0:T(8,128)(2,1)S(1)} collective-permute-done((bf16[8,8,16,896]{3,2,1,0:T(8,128)(2,1)S(1)}, bf16[8,8,16,896]{3,2,1,0:T(8,128)(2,1)S(1)}, u32[]{:S(2)}, u32[]{:S(2)}) %collective-permute-start.11) | collective-permute-done | bytes 1835040 | tf_op jit(solution)/shard_map/ppermute | solution.py:259
  181.1 13.8 %step.1 = (bf16[512,896]{1,0:T(8,128)(2,1)}, bf16[8,224,896]{2,1,0:T(8,128)(2,1)}) custom-call(s32[8]{0:T(128)S(1)} %stack.86.tab, f32[1]{0:T(128)} %bitcast.12.rate, bf16[8,224,512]{2,1,0:T(8,128)(2,1)} %all-to-all-done.2.tokens, bf16[8,224,896]{2,1,0:T(8,128)(2,1)} %all-to-all-done.own, bf16[512,896]{1,0:T(8,128)(2,1)S(1)} %bitcast.44, ...), custom_call_target="tpu_custom_call" | custom-call | flops 3288334336 | bytes 20000000 | tf_op jit(solution)/shard_map/step/pallas_call | solution.py:224
  194.9 7.3 %all-to-all-start.3 = ((bf16[8,224,896]{2,1,0:T(8,128)(2,1)}), bf16[8,224,896]{2,1,0:T(8,128)(2,1)}, u32[]{:S(2)}, u32[]{:S(2)}) async-start(bf16[8,224,896]{2,1,0:T(8,128)(2,1)} %get-tuple-element.29), calls=%async_computation.5 | async-start | bytes 6422528 | tf_op jit(solution)/shard_map/all_to_all | solution.py:352
  202.2 12.2 %all-gather.2.cloned.1.call-done.gathered = bf16[8,2,112,896]{3,2,1,0:T(8,128)(2,1)} async-done(((bf16[1,2,112,896]{3,2,1,0:T(8,128)(2,1)}), bf16[8,2,112,896]{3,2,1,0:T(8,128)(2,1)}) %all-gather.2.cloned.1.call-update) | async-done | bytes 3211280 | tf_op jit(solution)/shard_map/all_gather | solution.py:276
  214.3 2.8 %dynamic-slice_bitcast_fusion = bf16[8,112,896]{2,1,0:T(8,128)(2,1)} fusion(bf16[8,2,112,896]{3,2,1,0:T(8,128)(2,1)} %all-gather.2.cloned.1.call-done.gathered, s32[]{:T(128)S(6)} %select_n.28), kind=kLoop, calls=%fused_computation | loop fusion | bytes 3211268 | tf_op jit(solution)/shard_map/jit(dynamic_index_in_dim)/squeeze | solution.py:353
  217.1 31.0 %all-to-all-done.3.back = bf16[8,224,896]{2,1,0:T(8,128)(2,1)} async-done(((bf16[8,224,896]{2,1,0:T(8,128)(2,1)}), bf16[8,224,896]{2,1,0:T(8,128)(2,1)}, u32[]{:S(2)}, u32[]{:S(2)}) %all-to-all-start.3) | async-done | bytes 3211296 | tf_op jit(solution)/shard_map/all_to_all | solution.py:352
  248.1 6.6 %final.1 = bf16[224,7168]{1,0:T(8,128)(2,1)} custom-call(s32[8]{0:T(128)S(1)} %stack.86.tab, f32[1]{0:T(128)} %bitcast.12.rate, bf16[224,7168]{1,0:T(8,128)(2,1)S(1)} %bitcast.41, bf16[8,2,112,896]{3,2,1,0:T(8,128)(2,1)} %all-gather.2.cloned.1.call-done.gathered, bf16[8,112,896]{2,1,0:T(8,128)(2,1)} %collective-permute-done.12.received, ...), custom_call_target="tpu_custom_call" | custom-call | flops 5000000 | bytes 13000000 | tf_op jit(solution)/shard_map/final/pallas_call | solution.py:138
  (102 shorter events, 21.6 us)
Async XLA Ops:
  7.2 73.7 %reduce-scatter.3.cloned.1.call-start = ((), (), s32[]{:S(2)}) async-start(), calls=%async_computation.6 | async-start | bytes 4128768 | tf_op jit(solution)/shard_map/reduce_scatter | solution.py:272
  10.1 6.1 %collective-permute-start = (bf16[112,7168]{1,0:T(8,128)(2,1)}, bf16[112,7168]{1,0:T(8,128)(2,1)}, u32[]{:S(2)}, u32[]{:S(2)}) collective-permute-start(bf16[112,7168]{1,0:T(8,128)(2,1)} %dynamic-slice_bitcast_fusion.2), channel_id=1, source_target_pairs={{0,8},{8,0},{1,9},{9,1},{2,10},{10,2},{3,11},{11,3},{4,12},{12,4},... | collective-permute-start | bytes 4816904 | tf_op jit(solution)/shard_map/ppermute | solution.py:259
  25.3 55.6 %all-to-all-start = ((bf16[8,224,896]{2,1,0:T(8,128)(2,1)}), bf16[8,224,896]{2,1,0:T(8,128)(2,1)}, u32[]{:S(2)}, u32[]{:S(2)}) async-start(bf16[8,224,896]{2,1,0:T(8,128)(2,1)} %copy-done.3), calls=%async_computation.1 | async-start | bytes 6422528 | tf_op jit(solution)/shard_map/all_to_all | solution.py:327
  33.0 115.1 %reduce-scatter.5.cloned.1.call-start = ((), (), s32[]{:S(2)}) async-start(), calls=%async_computation.7 | async-start | bytes 3612672 | tf_op jit(solution)/shard_map/reduce_scatter | solution.py:272
  33.2 3.5 %collective-permute-start.1 = (bf16[112,7168]{1,0:T(8,128)(2,1)S(1)}, bf16[112,7168]{1,0:T(8,128)(2,1)S(1)}, u32[]{:S(2)}, u32[]{:S(2)}) collective-permute-start(bf16[112,7168]{1,0:T(8,128)(2,1)S(1)} %dynamic-slice_bitcast_fusion.1), channel_id=1, source_target_pairs={{0,8},{8,0},{1,9},{9,1},{2,10},{10,2},{3,11},{11,3},{4,12},{12,4},... | collective-permute-start | bytes 4816904 | tf_op jit(solution)/shard_map/ppermute | solution.py:259
  101.8 68.7 %copy-start.6 = (bf16[8,2,16,896]{3,2,1,0:T(8,128)(2,1)}, bf16[8,2,16,896]{3,2,1,0:T(8,128)(2,1)S(1)}, u32[]{:S(2)}) copy-start(bf16[8,2,16,896]{3,2,1,0:T(8,128)(2,1)S(1)} %slice_add_fusion.refs_0_) | copy-start | bytes 1376260
  103.2 44.9 %all-to-all-start.2 = ((bf16[8,224,512]{2,1,0:T(8,128)(2,1)}), bf16[8,224,512]{2,1,0:T(8,128)(2,1)}, u32[]{:S(2)}, u32[]{:S(2)}) async-start(bf16[8,224,512]{2,1,0:T(8,128)(2,1)} %broadcast_in_dim.33), calls=%async_computation.4 | async-start | bytes 3670016 | tf_op jit(solution)/shard_map/all_to_all | solution.py:339
  109.9 104.4 %all-gather.2.cloned.1.call-start = ((), (), s32[]{:S(2)}) async-start(), calls=%async_computation.8 | async-start | bytes 3612672 | tf_op jit(solution)/shard_map/all_gather | solution.py:276
  109.9 26.1 %collective-permute-start.2 = (bf16[8,2,16,896]{3,2,1,0:T(8,128)(2,1)S(1)}, bf16[8,2,16,896]{3,2,1,0:T(8,128)(2,1)S(1)}, u32[]{:S(2)}, u32[]{:S(2)}) collective-permute-start(bf16[8,2,16,896]{3,2,1,0:T(8,128)(2,1)S(1)} %slice_add_fusion.refs_0_), channel_id=1, source_target_pairs={{0,32},{32,64},{64,96},{96,128},{128,160},{160,192},{192,224},{224... | collective-permute-start | bytes 1376264 | tf_op jit(solution)/shard_map/ppermute | solution.py:285
  111.8 24.1 %collective-permute-start.4 = (bf16[8,2,16,896]{3,2,1,0:T(8,128)(2,1)S(1)}, bf16[8,2,16,896]{3,2,1,0:T(8,128)(2,1)S(1)}, u32[]{:S(2)}, u32[]{:S(2)}) collective-permute-start(bf16[8,2,16,896]{3,2,1,0:T(8,128)(2,1)S(1)} %slice_add_fusion.refs_0_), channel_id=1, source_target_pairs={{0,224},{32,0},{64,32},{96,64},{128,96},{160,128},{192,160},{224,1... | collective-permute-start | bytes 1376264 | tf_op jit(solution)/shard_map/ppermute | solution.py:285
  135.9 34.6 %copy-start.12 = (bf16[8,2,16,896]{3,2,1,0:T(8,128)(2,1)}, bf16[8,2,16,896]{3,2,1,0:T(8,128)(2,1)S(1)}, u32[]{:S(2)}) copy-start(bf16[8,2,16,896]{3,2,1,0:T(8,128)(2,1)S(1)} %collective-permute-done.2.refs_1_) | copy-start | bytes 1376260
  135.9 12.1 %collective-permute-start.3 = (bf16[8,2,16,896]{3,2,1,0:T(8,128)(2,1)S(1)}, bf16[8,2,16,896]{3,2,1,0:T(8,128)(2,1)S(1)}, u32[]{:S(2)}, u32[]{:S(2)}) collective-permute-start(bf16[8,2,16,896]{3,2,1,0:T(8,128)(2,1)S(1)} %collective-permute-done.2.refs_1_), channel_id=1, source_target_pairs={{0,32},{32,64},{64,96},{96,128},{128,160},{160,192},{192,224},{224... | collective-permute-start | bytes 1376264 | tf_op jit(solution)/shard_map/ppermute | solution.py:285
  135.9 34.6 %copy-start.14 = (bf16[8,2,16,896]{3,2,1,0:T(8,128)(2,1)}, bf16[8,2,16,896]{3,2,1,0:T(8,128)(2,1)S(1)}, u32[]{:S(2)}) copy-start(bf16[8,2,16,896]{3,2,1,0:T(8,128)(2,1)S(1)} %collective-permute-done.4.refs_2_) | copy-start | bytes 1376260
  136.0 12.1 %collective-permute-start.5 = (bf16[8,2,16,896]{3,2,1,0:T(8,128)(2,1)S(1)}, bf16[8,2,16,896]{3,2,1,0:T(8,128)(2,1)S(1)}, u32[]{:S(2)}, u32[]{:S(2)}) collective-permute-start(bf16[8,2,16,896]{3,2,1,0:T(8,128)(2,1)S(1)} %collective-permute-done.4.refs_2_), channel_id=1, source_target_pairs={{0,224},{32,0},{64,32},{96,64},{128,96},{160,128},{192,160},{224,1... | collective-permute-start | bytes 1376264 | tf_op jit(solution)/shard_map/ppermute | solution.py:285
  148.1 27.6 %copy-start.16 = (bf16[8,2,16,896]{3,2,1,0:T(8,128)(2,1)}, bf16[8,2,16,896]{3,2,1,0:T(8,128)(2,1)S(1)}, u32[]{:S(2)}) copy-start(bf16[8,2,16,896]{3,2,1,0:T(8,128)(2,1)S(1)} %collective-permute-done.3.refs_3_) | copy-start | bytes 1376260
  148.1 10.2 %collective-permute-start.7 = (bf16[8,2,16,896]{3,2,1,0:T(8,128)(2,1)S(1)}, bf16[8,2,16,896]{3,2,1,0:T(8,128)(2,1)S(1)}, u32[]{:S(2)}, u32[]{:S(2)}) collective-permute-start(bf16[8,2,16,896]{3,2,1,0:T(8,128)(2,1)S(1)} %collective-permute-done.5.refs_4_), channel_id=1, source_target_pairs={{0,224},{32,0},{64,32},{96,64},{128,96},{160,128},{192,160},{224,1... | collective-permute-start | bytes 1376264 | tf_op jit(solution)/shard_map/ppermute | solution.py:285
  150.0 11.5 %collective-permute-start.6 = (bf16[8,2,16,896]{3,2,1,0:T(8,128)(2,1)S(1)}, bf16[8,2,16,896]{3,2,1,0:T(8,128)(2,1)S(1)}, u32[]{:S(2)}, u32[]{:S(2)}) collective-permute-start(bf16[8,2,16,896]{3,2,1,0:T(8,128)(2,1)S(1)} %collective-permute-done.3.refs_3_), channel_id=1, source_target_pairs={{0,32},{32,64},{64,96},{96,128},{128,160},{160,192},{192,224},{224... | collective-permute-start | bytes 1376264 | tf_op jit(solution)/shard_map/ppermute | solution.py:285
  150.2 18.6 %collective-permute-start.10 = (bf16[1,2,112,896]{3,2,1,0:T(8,128)(2,1)}, bf16[1,2,112,896]{3,2,1,0:T(8,128)(2,1)S(1)}, u32[]{:S(2)}, u32[]{:S(2)}) collective-permute-start(bf16[1,2,112,896]{3,2,1,0:T(8,128)(2,1)} %reduce-scatter.5.cloned.1.call-done), channel_id=1, source_target_pairs={{0,16},{16,0},{1,17},{17,1},{2,18},{18,2},{3,19},{19,3},{4,20},{20... | collective-permute-start | bytes 1204232 | tf_op jit(solution)/shard_map/ppermute | solution.py:263
  158.3 6.7 %collective-permute-start.9 = (bf16[4,2,16,896]{3,2,1,0:T(8,128)(2,1)S(1)}, bf16[4,2,16,896]{3,2,1,0:T(8,128)(2,1)S(1)}, u32[]{:S(2)}, u32[]{:S(2)}) collective-permute-start(bf16[4,2,16,896]{3,2,1,0:T(8,128)(2,1)S(1)} %slice.27), channel_id=1, source_target_pairs={{0,224},{32,0},{64,32},{96,64},{128,96},{160,128},{192,160},{224,1... | collective-permute-start | bytes 688136 | tf_op jit(solution)/shard_map/ppermute | solution.py:290
  161.5 7.3 %collective-permute-start.8 = (bf16[4,2,16,896]{3,2,1,0:T(8,128)(2,1)S(1)}, bf16[4,2,16,896]{3,2,1,0:T(8,128)(2,1)S(1)}, u32[]{:S(2)}, u32[]{:S(2)}) collective-permute-start(bf16[4,2,16,896]{3,2,1,0:T(8,128)(2,1)S(1)} %slice.26), channel_id=1, source_target_pairs={{0,32},{32,64},{64,96},{96,128},{128,160},{160,192},{192,224},{224... | collective-permute-start | bytes 688136 | tf_op jit(solution)/shard_map/ppermute | solution.py:290
  171.6 4.1 %collective-permute-start.11 = (bf16[8,8,16,896]{3,2,1,0:T(8,128)(2,1)S(1)}, bf16[8,8,16,896]{3,2,1,0:T(8,128)(2,1)S(1)}, u32[]{:S(2)}, u32[]{:S(2)}) collective-permute-start(bf16[8,8,16,896]{3,2,1,0:T(8,128)(2,1)S(1)} %bitcast_dynamic-update-slice_fusion), channel_id=1, source_target_pairs={{0,8},{8,0},{1,9},{9,1},{2,10},{10,2},{3,11},{11,3},{4,12},{12,4},... | collective-permute-start | bytes 5505032 | tf_op jit(solution)/shard_map/ppermute | solution.py:259
  194.9 53.2 %all-to-all-start.3 = ((bf16[8,224,896]{2,1,0:T(8,128)(2,1)}), bf16[8,224,896]{2,1,0:T(8,128)(2,1)}, u32[]{:S(2)}, u32[]{:S(2)}) async-start(bf16[8,224,896]{2,1,0:T(8,128)(2,1)} %get-tuple-element.29), calls=%async_computation.5 | async-start | bytes 6422528 | tf_op jit(solution)/shard_map/all_to_all | solution.py:352
  202.2 45.9 %copy-start.1 = (bf16[1,224,7168]{2,1,0:T(8,128)(2,1)S(1)}, bf16[1,224,7168]{2,1,0:T(8,128)(2,1)}, u32[]{:S(2)}) copy-start(bf16[1,224,7168]{2,1,0:T(8,128)(2,1)} %param.9) | copy-start | bytes 9633796
  217.1 31.0 %collective-permute-start.12 = (bf16[8,112,896]{2,1,0:T(8,128)(2,1)}, bf16[8,112,896]{2,1,0:T(8,128)(2,1)}, u32[]{:S(2)}, u32[]{:S(2)}) collective-permute-start(bf16[8,112,896]{2,1,0:T(8,128)(2,1)} %dynamic-slice_bitcast_fusion), channel_id=1, source_target_pairs={{0,8},{8,0},{1,9},{9,1},{2,10},{10,2},{3,11},{11,3},{4,12},{12,4},... | collective-permute-start | bytes 4816904 | tf_op jit(solution)/shard_map/ppermute | solution.py:259
  (23 other events, 140.0 us)
Sparse Core Ops, SparseCore 0:
  21.0 53.4 reduce-scatter.2
  81.0 59.3 reduce-scatter.4
  169.9 44.3 all-gather.1

commit v5 on v4

--- a/solution.py
+++ b/solution.py
@@ -15,6 +15,7 @@
 GELU_B = 0.044715
 
 MINE_A, MINE_B, THEIRS_A, THEIRS_B, CORE, LOSER, SLOT, PLANE = range(8)
+MINE_HERE, THEIRS_HERE, MINE_ACROSS, THEIRS_ACROSS, HALF_TP = range(8, 13)
 DISTANCES = (0, -1, 1, -2, 2, -3, 3, 4)
 
 
@@ -24,35 +25,52 @@
     )
 
 
-def slots_kernel(tab, mine, theirs, out):
-    pair, _, half, width = out.shape
-    zero = jnp.zeros((half, width), mine.dtype)
-    for j in range(pair):
+def across_kernel(tab, mine, theirs, out):
+    zero = jnp.zeros(mine.shape, mine.dtype)
+    out[...] = jnp.where(
+        tab[MINE_ACROSS] == 1, mine[...], jnp.where(tab[THEIRS_ACROSS] == 1, theirs[...], zero)
+    )
+
+
+def here_kernel(tab, mine, theirs, crossed, out):
+    width = out.shape[2]
+    for j in range(out.shape[0]):
         at = slice(j * width, (j + 1) * width)
-        for s, (own, other) in enumerate(((MINE_A, THEIRS_A), (MINE_B, THEIRS_B))):
-            out[j, s] = jnp.where(
-                tab[own] == 1, mine[:, at], jnp.where(tab[other] == 1, theirs[:, at], zero)
-            )
-
-
-def build_slots(tab, shard, theirs):
-    half, width = shard.shape[0] // 2, shard.shape[1] // NZ
+        out[j] = jnp.where(
+            tab[MINE_HERE] == 1,
+            mine[:, at],
+            jnp.where(tab[THEIRS_HERE] == 1, theirs[:, at], crossed[:, at]),
+        )
+
+
+def one_slot(kernel, tab, shard, halves, out_spec, out_shape, name):
+    half, width = shard.shape[0] // 2, PAIR * shard.shape[1] // NZ
     return pl.pallas_call(
-        slots_kernel,
+        kernel,
         grid_spec=pltpu.PrefetchScalarGridSpec(
             num_scalar_prefetch=1,
             grid=(NZ // PAIR,),
-            in_specs=[
-                pl.BlockSpec((half, PAIR * width), lambda j, tab: (tab[CORE], j)),
-                pl.BlockSpec((half, PAIR * width), lambda j, tab: (0, j)),
-            ],
-            out_specs=pl.BlockSpec((PAIR, 2, half, width), lambda j, tab: (j, 0, 0, 0)),
+            in_specs=[pl.BlockSpec((half, width), lambda j, tab: (tab[CORE], j))]
+            + [pl.BlockSpec((half, width), lambda j, tab: (0, j))] * len(halves),
+            out_specs=out_spec,
         ),
-        out_shape=jax.ShapeDtypeStruct((NZ, 2, half, width), shard.dtype),
+        out_shape=jax.ShapeDtypeStruct(out_shape, shard.dtype),
         compiler_params=params(),
-        cost_estimate=pl.CostEstimate(flops=5_000_000, bytes_accessed=10_000_000, transcendentals=0),
-        name="slots",
-    )(tab, shard, theirs)
+        cost_estimate=pl.CostEstimate(flops=2_000_000, bytes_accessed=5_000_000, transcendentals=0),
+        name=name,
+    )(tab, shard, *halves)
+
+
+def slot_across(tab, shard, theirs):
+    half, width = shard.shape[0] // 2, PAIR * shard.shape[1] // NZ
+    spec = pl.BlockSpec((half, width), lambda j, tab: (0, j))
+    return one_slot(across_kernel, tab, shard, (theirs,), spec, (half, shard.shape[1]), "across")
+
+
+def slot_here(tab, shard, theirs, crossed):
+    half, width = shard.shape[0] // 2, shard.shape[1] // NZ
+    spec = pl.BlockSpec((PAIR, half, width), lambda j, tab: (j, 0, 0))
+    return one_slot(here_kernel, tab, shard, (theirs, crossed), spec, (NZ, half, width), "here")
 
 
 def row_slots_kernel(tab, mine, theirs, out):
@@ -160,6 +178,7 @@
     i = pl.program_id(0)
     steps = NK // PAIR
     pair = lax.rem(i, steps) * PAIR
+    near_k = lax.rem(pair + (NK // 2) * tab[HALF_TP], NK)
     half = own.shape[1] // 2
     width = own.shape[2]
 
@@ -177,7 +196,7 @@
                     weight[pair + p, pl.ds(near, ROWS)] = gathered[n][p, 0]
                     weight[pair + p, pl.ds(far, ROWS)] = received[n, p]
 
-        t = tokens[pl.ds(pair, PAIR)].reshape(PAIR * 2 * half, -1)
+        t = tokens[pl.ds(near_k, PAIR)].reshape(PAIR * 2 * half, -1)
         w = weight[pl.ds(pair, PAIR)].reshape(PAIR * 2 * half, width)
         part = lax.dot_general(t, w, (((0,), (0,)), ((), ())), preferred_element_type=jnp.float32)
 
@@ -206,7 +225,7 @@
 
     @pl.when(i >= steps)
     def _():
-        t = tokens[pl.ds(pair, PAIR)].reshape(PAIR * 2 * half, -1)
+        t = tokens[pl.ds(near_k, PAIR)].reshape(PAIR * 2 * half, -1)
         gw = jnp.dot(t, grad[...], preferred_element_type=jnp.float32)
         w = weight[pl.ds(pair, PAIR)].reshape(PAIR * 2 * half, width)
         back[...] = (w.astype(jnp.float32) - rate[0] * gw).astype(back.dtype).reshape(back.shape)
@@ -297,6 +316,8 @@
     partner = me + 1 - 2 * core
     loser_ids, winner_ids = assignment[:, 0], assignment[:, 1]
     win_a, win_b = jnp.min(winner_ids), jnp.max(winner_ids)
+    left = lax.axis_index("yl") == 0
+    here, across = jnp.where(left, win_a, win_b), jnp.where(left, win_b, win_a)
 
     def slot_of(member):
         hit = loser_ids == member
@@ -314,6 +335,11 @@
             loser.astype(jnp.int32),
             slot,
             lax.axis_index("z").astype(jnp.int32),
+            (here == me).astype(jnp.int32),
+            (here == partner).astype(jnp.int32),
+            (across == me).astype(jnp.int32),
+            (across == partner).astype(jnp.int32),
+            lax.axis_index("yh").astype(jnp.int32),
         ]
     )
     member_ids = jnp.arange(lr_index.shape[0], dtype=jnp.int32)
@@ -324,30 +350,40 @@
     w, m = weight[0], momentum[0]
     w_slots = build_row_slots(tab, w, partner_rows(w, core))
     w_mine = scatter(w_slots)
-    own_columns = lax.all_to_all(column_blocks(w), TP, 0, 0, tiled=True)
-    m_slots = build_slots(tab, m, partner_rows(m, core))
-    w_mine, own_columns, m_slots, rate = lax.optimization_barrier(
-        (w_mine, own_columns, m_slots, rate)
-    )
-    m_mine = scatter(m_slots)
+    m, tokens, w_slots = lax.optimization_barrier((m, tokens, w_slots))
+    m_theirs = partner_rows(m, core)
+    m_cross = slot_across(tab, m, m_theirs)
+    m_cross, tokens = lax.optimization_barrier((m_cross, tokens))
+    turned = jnp.swapaxes(tokens, 1, 2)
+    turned = jnp.broadcast_to(turned, (NK // 2,) + turned.shape[1:])
+    near_tokens = lax.all_to_all(turned, "x", 0, 0, tiled=True)
+    m_slot = slot_here(tab, m, m_theirs, swap_column(m_cross))
+    w_blocks = column_blocks(w)
+    w_mine, m_slot, w_blocks, near_tokens, rate = lax.optimization_barrier(
+        (w_mine, m_slot, w_blocks, near_tokens, rate)
+    )
+    m_mine = scatter(m_slot)[0]
     both = jnp.broadcast_to(w_mine, (2,) + w_mine.shape[1:])
     both = both.reshape((2 * NK,) + w_mine.shape[2:])
     both = lax.all_to_all(both, ("yl",) + TP, 0, 0, tiled=True)
     w_mine = both[:NK] + both[NK:]
-    turned = jnp.swapaxes(tokens, 1, 2)
-    w_mine, turned = lax.optimization_barrier((w_mine, turned))
-    all_tokens = lax.all_to_all(
-        jnp.broadcast_to(turned, (NK,) + turned.shape[1:]), TP, 0, 0, tiled=True
-    )
-    pieces, (m_mine, all_tokens) = ring(w_mine, (m_mine, all_tokens))
+    w_mine, w_blocks, near_tokens = lax.optimization_barrier((w_mine, w_blocks, near_tokens))
+    own_columns = lax.all_to_all(w_blocks, TP, 0, 0, tiled=True)
+    far_tokens = lax.ppermute(near_tokens, "yh", [(0, 1), (1, 0)])
+    pieces, m_mine = ring(w_mine, m_mine)
+
     m_across = swap_column(m_mine)
-    pieces[-1], m_across = lax.optimization_barrier((pieces[-1], m_across))
+    pieces[-1], own_columns, far_tokens, m_across = lax.optimization_barrier(
+        (pieces[-1], own_columns, far_tokens, m_across)
+    )
+    all_tokens = jnp.concatenate([near_tokens, far_tokens])
     w_other = swap_core(
         jnp.stack(
             [lax.dynamic_index_in_dim(p, partner_slot, axis=1, keepdims=False) for p in pieces]
         )
     )
-    m_won = gather(m_mine + m_across)
+    m_mine = jnp.where(left, jnp.stack([m_mine, m_across]), jnp.stack([m_across, m_mine]))
+    m_won = gather(m_mine[None])
     activation, back = step(tab, rate, all_tokens, own_columns, cotangent[0], w_other, pieces)
     back = lax.all_to_all(back, TP, 0, 0, tiled=True)
     m_other = swap_core(lax.dynamic_index_in_dim(m_won, partner_slot, axis=1, keepdims=False))

time: 263 us -> 256 us (0.973)
  waiting for transfers between devices: 131 us -> 117 us
  local copies, waits for them, and re-layouts: 16.9 us -> 12.2 us
  Pallas kernels: 32.5 us -> 36.5 us
  other arithmetic: 4.93 us -> 8.89 us
    all_to_all x2, waiting for transfers between devices: 39.5 us -> 0.01 us  [the longest x1 0.01 us: local(): near_tokens = lax.all_to_all(turned, 'x', 0, 0, tiled=True)]
    ppermute x1 -> x2, waiting for transfers between devices: 0.01 us -> 25.4 us  [swap_column(): return lax.ppermute(x, 'yl', [(0, 1), (1, 0)])]
    ppermute x6, waiting for transfers between devices: 35.6 us -> 27.9 us  [ring(): low, high = (lax.ppermute(low, 'z', up), lax.ppermute(high, 'z', down))]
    ppermute x0 -> x1, waiting for transfers between devices: none -> 5.7 us  [local(): far_tokens = lax.ppermute(near_tokens, 'yh', [(0, 1), (1, 0)])]
    unnamed x63 -> x33, local copies, waits for them, and re-layouts: 9.53 us -> 5.28 us
    all_gather x1, waiting for transfers between devices: 12.2 us -> 16.2 us  [gather(): return lax.all_gather(mine, 'z', axis=0, tiled=True)]
    ppermute x0 -> x1, starting transfers between devices: none -> 2.99 us  [local(): far_tokens = lax.ppermute(near_tokens, 'yh', [(0, 1), (1, 0)])]
    all_to_all x1, waiting for transfers between devices: 31 us -> 28.1 us  [local(): back = lax.all_to_all(back, TP, 0, 0, tiled=True)]
  transfers between devices with their start and end apart: 19 -> 21, of which waited for: 10 -> 13; matrix products, arithmetic and copies ran while one was open for 3% -> 4% of each run, Pallas kernels for 8% -> 10%
where the time goes in v5:
time: 256 us; the launch traced here: 255 us
  waiting for transfers between devices  117 us (46%)
  starting transfers between devices  39.2 us (15%)
  Pallas kernels  36.5 us (14%)
  between operations  21.2 us (8%)
  blocking collectives  20.4 us (8%)
  local copies, waits for them, and re-layouts  12.2 us (5%)
  other arithmetic  8.89 us (3%)
    all_to_all x1, waiting for transfers between devices, local(): back = lax.all_to_all(back, TP, 0, 0, tiled=True)  28.1 us
    ppermute x6, waiting for transfers between devices, ring(): low, high = (lax.ppermute(low, 'z', up), lax.ppermute(high, 'z', down))  27.9 us
    ppermute x2, waiting for transfers between devices, swap_column(): return lax.ppermute(x, 'yl', [(0, 1), (1, 0)])  25.4 us
    all_to_all x1, blocking collectives, local(): both = lax.all_to_all(both, ('yl',) + TP, 0, 0, tiled=True)  20.4 us
    all_gather x1, waiting for transfers between devices, gather(): return lax.all_gather(mine, 'z', axis=0, tiled=True)  16.2 us
    pallas_call x1, Pallas kernels, step(): pl.pallas_call(step_kernel, grid_spec=pltpu.PrefetchScalarGridSpec(num_sc...  13.6 us
    ppermute x6, starting transfers between devices, ring(): low, high = (lax.ppermute(low, 'z', up), lax.ppermute(high, 'z', down))  9.88 us
    all_to_all x1, starting transfers between devices, local(): back = lax.all_to_all(back, TP, 0, 0, tiled=True)  7.65 us
  transfers between devices with their start and end apart: 21, of which 13 were waited for; matrix products, arithmetic and copies ran while one was open for 4% of the time, Pallas kernels for 10%

profile of v5, /device:TPU:6, one launch (start us, length us, event | category | flops | bytes accessed | tf_op | source)
XLA Modules:
  0.0 255.4 jit_solution(1756477318241406022)
XLA Ops:
  19.0 4.6 %row_slots.1 = bf16[8,8,2,16,896]{4,3,2,1,0:T(8,128)(2,1)} custom-call(s32[13]{0:T(128)S(1)} %stack.136.tab, bf16[224,7168]{1,0:T(8,128)(2,1)S(1)} %bitcast.52, bf16[112,7168]{1,0:T(8,128)(2,1)} %collective-permute-done.theirs), custom_call_target="tpu_custom_call" | custom-call | flops 5000000 | bytes 10000000 | tf_op jit(solution)/shard_map/row_slots/pallas_call | solution.py:93
  26.3 3.1 %collective-permute-done.1.theirs = bf16[112,7168]{1,0:T(8,128)(2,1)S(1)} collective-permute-done((bf16[112,7168]{1,0:T(8,128)(2,1)S(1)}, bf16[112,7168]{1,0:T(8,128)(2,1)S(1)}, u32[]{:S(2)}, u32[]{:S(2)}) %collective-permute-start.1) | collective-permute-done | bytes 1605664 | tf_op jit(solution)/shard_map/ppermute | solution.py:278
  29.4 2.9 %across.1 = bf16[112,7168]{1,0:T(8,128)(2,1)S(1)} custom-call(s32[13]{0:T(128)S(1)} %stack.136.tab, bf16[224,7168]{1,0:T(8,128)(2,1)} %bitcast.47, bf16[112,7168]{1,0:T(8,128)(2,1)S(1)} %collective-permute-done.1.theirs), custom_call_target="tpu_custom_call" | custom-call | flops 2000000 | bytes 5000000 | tf_op jit(solution)/shard_map/across/pallas_call | solution.py:48
  34.9 4.8 %all-to-all-start = ((bf16[4,224,512]{2,1,0:T(8,128)(2,1)}), bf16[4,224,512]{2,1,0:T(8,128)(2,1)}, u32[]{:S(2)}, u32[]{:S(2)}) async-start(bf16[4,224,512]{2,1,0:T(8,128)(2,1)} %broadcast_in_dim.30), calls=%async_computation.1 | async-start | bytes 1835008 | tf_op jit(solution)/shard_map/all_to_all | solution.py:359
  39.8 4.2 %column_blocks.1 = bf16[8,224,896]{2,1,0:T(8,128)(2,1)} custom-call(bf16[224,7168]{1,0:T(8,128)(2,1)} %bitcast.51), custom_call_target="tpu_custom_call" | custom-call | flops 1000000 | bytes 6400000 | tf_op jit(solution)/shard_map/column_blocks/pallas_call | solution.py:119
  45.9 23.9 %collective-permute-done.2.crossed = bf16[112,7168]{1,0:T(8,128)(2,1)} collective-permute-done((bf16[112,7168]{1,0:T(8,128)(2,1)S(1)}, bf16[112,7168]{1,0:T(8,128)(2,1)}, u32[]{:S(2)}, u32[]{:S(2)}) %collective-permute-start.2) | collective-permute-done | bytes 1605664 | tf_op jit(solution)/shard_map/ppermute | solution.py:282
  69.8 4.5 %here.1 = bf16[8,112,896]{2,1,0:T(8,128)(2,1)} custom-call(s32[13]{0:T(128)S(1)} %stack.136.tab, bf16[224,7168]{1,0:T(8,128)(2,1)} %bitcast.48, bf16[112,7168]{1,0:T(8,128)(2,1)S(1)} %collective-permute-done.1.theirs, bf16[112,7168]{1,0:T(8,128)(2,1)} %collective-permute-done.2.crossed), custom_call_target="tpu_custom_call" | custom-call | flops 2000000 | bytes 5000000 | tf_op jit(solution)/shard_map/here/pallas_call | solution.py:48
  74.3 2.9 %reduce-scatter.3.cloned.1.call-done = bf16[1,8,2,16,896]{4,3,2,1,0:T(8,128)(2,1)} async-done(((bf16[8,8,2,16,896]{4,3,2,1,0:T(8,128)(2,1)}), bf16[1,8,2,16,896]{4,3,2,1,0:T(8,128)(2,1)}) %reduce-scatter.3.cloned.1.call-update) | async-done | bytes 458768 | tf_op jit(solution)/shard_map/reduce_scatter | solution.py:291
  78.4 20.4 %all_to_all.20 = bf16[16,2,16,896]{3,2,1,0:T(8,128)(2,1)S(1)} all-to-all(bf16[16,2,16,896]{3,2,1,0:T(8,128)(2,1)S(1)} %bitcast.54), channel_id=1, replica_groups=mesh['z'=8,'yl'=2,'c'=2,'yh'=2,'x'=4] {'yl','yh','x'}, dimensions={0} | all-to-all | bytes 1835008 | tf_op jit(solution)/shard_map/all_to_all | solution.py:368
  98.8 6.8 %all-to-all-start.2 = ((bf16[8,224,896]{2,1,0:T(8,128)(2,1)}), bf16[8,224,896]{2,1,0:T(8,128)(2,1)}, u32[]{:S(2)}, u32[]{:S(2)}) async-start(bf16[8,224,896]{2,1,0:T(8,128)(2,1)} %column_blocks.1), calls=%async_computation.4 | async-start | bytes 6422528 | tf_op jit(solution)/shard_map/all_to_all | solution.py:371
  105.6 3.2 %collective-permute-start.5 = (bf16[8,2,16,896]{3,2,1,0:T(8,128)(2,1)S(1)}, bf16[8,2,16,896]{3,2,1,0:T(8,128)(2,1)S(1)}, u32[]{:S(2)}, u32[]{:S(2)}) collective-permute-start(bf16[8,2,16,896]{3,2,1,0:T(8,128)(2,1)S(1)} %slice_add_fusion.refs_0_), channel_id=1, source_target_pairs={{0,224},{32,0},{64,32},{96,64},{128,96},{160,128},{192,160},{224,1... | collective-permute-start | bytes 1376264 | tf_op jit(solution)/shard_map/ppermute | solution.py:304
  108.8 14.3 %collective-permute-done.3.refs_1_ = bf16[8,2,16,896]{3,2,1,0:T(8,128)(2,1)S(1)} collective-permute-done((bf16[8,2,16,896]{3,2,1,0:T(8,128)(2,1)S(1)}, bf16[8,2,16,896]{3,2,1,0:T(8,128)(2,1)S(1)}, u32[]{:S(2)}, u32[]{:S(2)}) %collective-permute-start.3) | collective-permute-done | bytes 458784 | tf_op jit(solution)/shard_map/ppermute | solution.py:304
  126.4 3.0 %collective-permute-start.11 = (bf16[4,224,512]{2,1,0:T(8,128)(2,1)}, bf16[4,224,512]{2,1,0:T(8,128)(2,1)}, u32[]{:S(2)}, u32[]{:S(2)}) collective-permute-start(bf16[4,224,512]{2,1,0:T(8,128)(2,1)} %all-to-all-done), channel_id=1, source_target_pairs={{0,4},{4,0},{1,5},{5,1},{2,6},{6,2},{3,7},{7,3},{8,12},{12,8},{9,1... | collective-permute-start | bytes 2752520 | tf_op jit(solution)/shard_map/ppermute | solution.py:372
  129.4 5.8 %collective-permute-done.4.refs_3_ = bf16[8,2,16,896]{3,2,1,0:T(8,128)(2,1)S(1)} collective-permute-done((bf16[8,2,16,896]{3,2,1,0:T(8,128)(2,1)S(1)}, bf16[8,2,16,896]{3,2,1,0:T(8,128)(2,1)S(1)}, u32[]{:S(2)}, u32[]{:S(2)}) %collective-permute-start.4) | collective-permute-done | bytes 458784 | tf_op jit(solution)/shard_map/ppermute | solution.py:304
  135.2 3.4 %collective-permute-start.9 = (bf16[8,2,16,896]{3,2,1,0:T(8,128)(2,1)S(1)}, bf16[8,2,16,896]{3,2,1,0:T(8,128)(2,1)S(1)}, u32[]{:S(2)}, u32[]{:S(2)}) collective-permute-start(bf16[8,2,16,896]{3,2,1,0:T(8,128)(2,1)S(1)} %collective-permute-done.6.refs_4_), channel_id=1, source_target_pairs={{0,224},{32,0},{64,32},{96,64},{128,96},{160,128},{192,160},{224,1... | collective-permute-start | bytes 1376264 | tf_op jit(solution)/shard_map/ppermute | solution.py:304
  138.6 7.8 %collective-permute-done.9.refs_6_ = bf16[8,2,16,896]{3,2,1,0:T(8,128)(2,1)S(1)} collective-permute-done((bf16[8,2,16,896]{3,2,1,0:T(8,128)(2,1)S(1)}, bf16[8,2,16,896]{3,2,1,0:T(8,128)(2,1)S(1)}, u32[]{:S(2)}, u32[]{:S(2)}) %collective-permute-start.9) | collective-permute-done | bytes 458784 | tf_op jit(solution)/shard_map/ppermute | solution.py:304
  146.4 3.8 %collective-permute-start.10 = (bf16[4,2,16,896]{3,2,1,0:T(8,128)(2,1)S(1)}, bf16[4,2,16,896]{3,2,1,0:T(8,128)(2,1)S(1)}, u32[]{:S(2)}, u32[]{:S(2)}) collective-permute-start(bf16[4,2,16,896]{3,2,1,0:T(8,128)(2,1)S(1)} %slice.27), channel_id=1, source_target_pairs={{0,224},{32,0},{64,32},{96,64},{128,96},{160,128},{192,160},{224,1... | collective-permute-start | bytes 688136 | tf_op jit(solution)/shard_map/ppermute | solution.py:309
  153.8 3.8 %collective-permute-done.8 = bf16[4,2,16,896]{3,2,1,0:T(8,128)(2,1)S(1)} collective-permute-done((bf16[4,2,16,896]{3,2,1,0:T(8,128)(2,1)S(1)}, bf16[4,2,16,896]{3,2,1,0:T(8,128)(2,1)S(1)}, u32[]{:S(2)}, u32[]{:S(2)}) %collective-permute-start.8) | collective-permute-done | bytes 229408 | tf_op jit(solution)/shard_map/ppermute | solution.py:309
  157.6 5.7 %collective-permute-done.11 = bf16[4,224,512]{2,1,0:T(8,128)(2,1)} collective-permute-done((bf16[4,224,512]{2,1,0:T(8,128)(2,1)}, bf16[4,224,512]{2,1,0:T(8,128)(2,1)}, u32[]{:S(2)}, u32[]{:S(2)}) %collective-permute-start.11) | collective-permute-done | bytes 917536 | tf_op jit(solution)/shard_map/ppermute | solution.py:372
  173.8 13.6 %step.1 = (bf16[512,896]{1,0:T(8,128)(2,1)}, bf16[8,224,896]{2,1,0:T(8,128)(2,1)}) custom-call(s32[13]{0:T(128)S(1)} %stack.136.tab, f32[1]{0:T(128)} %bitcast.18.rate, bf16[8,224,512]{2,1,0:T(8,128)(2,1)} %pad_maximum_fusion.tokens, bf16[8,224,896]{2,1,0:T(8,128)(2,1)} %all-to-all-done.2.own, bf16[512,896]{1,0:T(8,128)(2,1)S(1)} %bitcast.53, ...), custom_call_target="tpu_custom_call" | custom-call | flops 3288334336 | bytes 20000000 | tf_op jit(solution)/shard_map/step/pallas_call | solution.py:243
  187.4 7.7 %all-to-all-start.3 = ((bf16[8,224,896]{2,1,0:T(8,128)(2,1)}), bf16[8,224,896]{2,1,0:T(8,128)(2,1)}, u32[]{:S(2)}, u32[]{:S(2)}) async-start(bf16[8,224,896]{2,1,0:T(8,128)(2,1)} %get-tuple-element.43), calls=%async_computation.5 | async-start | bytes 6422528 | tf_op jit(solution)/shard_map/all_to_all | solution.py:388
  195.0 16.2 %all-gather.2.cloned.1.call-done.gathered = bf16[8,2,112,896]{3,2,1,0:T(8,128)(2,1)} async-done(((bf16[1,2,112,896]{3,2,1,0:T(8,128)(2,1)}), bf16[8,2,112,896]{3,2,1,0:T(8,128)(2,1)}) %all-gather.2.cloned.1.call-update) | async-done | bytes 3211280 | tf_op jit(solution)/shard_map/all_gather | solution.py:295
  214.1 28.1 %all-to-all-done.3.back = bf16[8,224,896]{2,1,0:T(8,128)(2,1)} async-done(((bf16[8,224,896]{2,1,0:T(8,128)(2,1)}), bf16[8,224,896]{2,1,0:T(8,128)(2,1)}, u32[]{:S(2)}, u32[]{:S(2)}) %all-to-all-start.3) | async-done | bytes 3211296 | tf_op jit(solution)/shard_map/all_to_all | solution.py:388
  242.2 6.7 %final.1 = bf16[224,7168]{1,0:T(8,128)(2,1)} custom-call(s32[13]{0:T(128)S(1)} %stack.136.tab, f32[1]{0:T(128)} %bitcast.18.rate, bf16[224,7168]{1,0:T(8,128)(2,1)S(1)} %bitcast.50, bf16[8,2,112,896]{3,2,1,0:T(8,128)(2,1)} %all-gather.2.cloned.1.call-done.gathered, bf16[8,112,896]{2,1,0:T(8,128)(2,1)} %collective-permute-done.14.received, ...), custom_call_target="tpu_custom_call" | custom-call | flops 5000000 | bytes 13000000 | tf_op jit(solution)/shard_map/final/pallas_call | solution.py:156
  (78 shorter events, 32.9 us)
Async XLA Ops:
  7.2 70.1 %reduce-scatter.3.cloned.1.call-start = ((), (), s32[]{:S(2)}) async-start(), calls=%async_computation.6 | async-start | bytes 4128768 | tf_op jit(solution)/shard_map/reduce_scatter | solution.py:291
  10.1 8.9 %collective-permute-start = (bf16[112,7168]{1,0:T(8,128)(2,1)}, bf16[112,7168]{1,0:T(8,128)(2,1)}, u32[]{:S(2)}, u32[]{:S(2)}) collective-permute-start(bf16[112,7168]{1,0:T(8,128)(2,1)} %dynamic-slice_bitcast_fusion.1), channel_id=1, source_target_pairs={{0,8},{8,0},{1,9},{9,1},{2,10},{10,2},{3,11},{11,3},{4,12},{12,4},... | collective-permute-start | bytes 4816904 | tf_op jit(solution)/shard_map/ppermute | solution.py:278
  25.7 3.7 %collective-permute-start.1 = (bf16[112,7168]{1,0:T(8,128)(2,1)S(1)}, bf16[112,7168]{1,0:T(8,128)(2,1)S(1)}, u32[]{:S(2)}, u32[]{:S(2)}) collective-permute-start(bf16[112,7168]{1,0:T(8,128)(2,1)S(1)} %constant_dynamic-slice_fusion), channel_id=1, source_target_pairs={{0,8},{8,0},{1,9},{9,1},{2,10},{10,2},{3,11},{11,3},{4,12},{12,4},... | collective-permute-start | bytes 4816904 | tf_op jit(solution)/shard_map/ppermute | solution.py:278
  32.3 37.6 %collective-permute-start.2 = (bf16[112,7168]{1,0:T(8,128)(2,1)S(1)}, bf16[112,7168]{1,0:T(8,128)(2,1)}, u32[]{:S(2)}, u32[]{:S(2)}) collective-permute-start(bf16[112,7168]{1,0:T(8,128)(2,1)S(1)} %across.1), channel_id=1, source_target_pairs={{0,16},{16,0},{1,17},{17,1},{2,18},{18,2},{3,19},{19,3},{4,20},{20... | collective-permute-start | bytes 4816904 | tf_op jit(solution)/shard_map/ppermute | solution.py:282
  34.9 39.4 %all-to-all-start = ((bf16[4,224,512]{2,1,0:T(8,128)(2,1)}), bf16[4,224,512]{2,1,0:T(8,128)(2,1)}, u32[]{:S(2)}, u32[]{:S(2)}) async-start(bf16[4,224,512]{2,1,0:T(8,128)(2,1)} %broadcast_in_dim.30), calls=%async_computation.1 | async-start | bytes 1835008 | tf_op jit(solution)/shard_map/all_to_all | solution.py:359
  39.8 95.4 %reduce-scatter.5.cloned.1.call-start = ((), (), s32[]{:S(2)}) async-start(), calls=%async_computation.7 | async-start | bytes 1806336 | tf_op jit(solution)/shard_map/reduce_scatter | solution.py:291
  98.8 66.0 %all-to-all-start.2 = ((bf16[8,224,896]{2,1,0:T(8,128)(2,1)}), bf16[8,224,896]{2,1,0:T(8,128)(2,1)}, u32[]{:S(2)}, u32[]{:S(2)}) async-start(bf16[8,224,896]{2,1,0:T(8,128)(2,1)} %column_blocks.1), calls=%async_computation.4 | async-start | bytes 6422528 | tf_op jit(solution)/shard_map/all_to_all | solution.py:371
  105.6 105.7 %all-gather.2.cloned.1.call-start = ((), (), s32[]{:S(2)}) async-start(), calls=%async_computation.8 | async-start | bytes 3612672 | tf_op jit(solution)/shard_map/all_gather | solution.py:295
  105.6 17.5 %collective-permute-start.3 = (bf16[8,2,16,896]{3,2,1,0:T(8,128)(2,1)S(1)}, bf16[8,2,16,896]{3,2,1,0:T(8,128)(2,1)S(1)}, u32[]{:S(2)}, u32[]{:S(2)}) collective-permute-start(bf16[8,2,16,896]{3,2,1,0:T(8,128)(2,1)S(1)} %slice_add_fusion.refs_0_), channel_id=1, source_target_pairs={{0,32},{32,64},{64,96},{96,128},{128,160},{160,192},{192,224},{224... | collective-permute-start | bytes 1376264 | tf_op jit(solution)/shard_map/ppermute | solution.py:304
  105.6 18.0 %collective-permute-start.5 = (bf16[8,2,16,896]{3,2,1,0:T(8,128)(2,1)S(1)}, bf16[8,2,16,896]{3,2,1,0:T(8,128)(2,1)S(1)}, u32[]{:S(2)}, u32[]{:S(2)}) collective-permute-start(bf16[8,2,16,896]{3,2,1,0:T(8,128)(2,1)S(1)} %slice_add_fusion.refs_0_), channel_id=1, source_target_pairs={{0,224},{32,0},{64,32},{96,64},{128,96},{160,128},{192,160},{224,1... | collective-permute-start | bytes 1376264 | tf_op jit(solution)/shard_map/ppermute | solution.py:304
  123.1 12.1 %collective-permute-start.4 = (bf16[8,2,16,896]{3,2,1,0:T(8,128)(2,1)S(1)}, bf16[8,2,16,896]{3,2,1,0:T(8,128)(2,1)S(1)}, u32[]{:S(2)}, u32[]{:S(2)}) collective-permute-start(bf16[8,2,16,896]{3,2,1,0:T(8,128)(2,1)S(1)} %collective-permute-done.3.refs_1_), channel_id=1, source_target_pairs={{0,32},{32,64},{64,96},{96,128},{128,160},{160,192},{192,224},{224... | collective-permute-start | bytes 1376264 | tf_op jit(solution)/shard_map/ppermute | solution.py:304
  123.6 11.6 %collective-permute-start.6 = (bf16[8,2,16,896]{3,2,1,0:T(8,128)(2,1)S(1)}, bf16[8,2,16,896]{3,2,1,0:T(8,128)(2,1)S(1)}, u32[]{:S(2)}, u32[]{:S(2)}) collective-permute-start(bf16[8,2,16,896]{3,2,1,0:T(8,128)(2,1)S(1)} %collective-permute-done.5.refs_2_), channel_id=1, source_target_pairs={{0,224},{32,0},{64,32},{96,64},{128,96},{160,128},{192,160},{224,1... | collective-permute-start | bytes 1376264 | tf_op jit(solution)/shard_map/ppermute | solution.py:304
  126.4 36.9 %collective-permute-start.11 = (bf16[4,224,512]{2,1,0:T(8,128)(2,1)}, bf16[4,224,512]{2,1,0:T(8,128)(2,1)}, u32[]{:S(2)}, u32[]{:S(2)}) collective-permute-start(bf16[4,224,512]{2,1,0:T(8,128)(2,1)} %all-to-all-done), channel_id=1, source_target_pairs={{0,4},{4,0},{1,5},{5,1},{2,6},{6,2},{3,7},{7,3},{8,12},{12,8},{9,1... | collective-permute-start | bytes 2752520 | tf_op jit(solution)/shard_map/ppermute | solution.py:372
  135.2 18.6 %copy-start.3 = (bf16[8,2,16,896]{3,2,1,0:T(8,128)(2,1)}, bf16[8,2,16,896]{3,2,1,0:T(8,128)(2,1)S(1)}, u32[]{:S(2)}) copy-start(bf16[8,2,16,896]{3,2,1,0:T(8,128)(2,1)S(1)} %collective-permute-done.6.refs_4_) | copy-start | bytes 1376260
  135.2 29.6 %copy-start.8 = (bf16[1,112,896]{2,1,0:T(8,128)(2,1)S(1)}, bf16[1,112,896]{2,1,0:T(8,128)(2,1)}, u32[]{:S(2)}) copy-start(bf16[1,112,896]{2,1,0:T(8,128)(2,1)} %reduce-scatter.5.cloned.1.call-done) | copy-start | bytes 602116
  135.2 11.2 %collective-permute-start.9 = (bf16[8,2,16,896]{3,2,1,0:T(8,128)(2,1)S(1)}, bf16[8,2,16,896]{3,2,1,0:T(8,128)(2,1)S(1)}, u32[]{:S(2)}, u32[]{:S(2)}) collective-permute-start(bf16[8,2,16,896]{3,2,1,0:T(8,128)(2,1)S(1)} %collective-permute-done.6.refs_4_), channel_id=1, source_target_pairs={{0,224},{32,0},{64,32},{96,64},{128,96},{160,128},{192,160},{224,1... | collective-permute-start | bytes 1376264 | tf_op jit(solution)/shard_map/ppermute | solution.py:304
  138.6 11.6 %collective-permute-start.7 = (bf16[8,2,16,896]{3,2,1,0:T(8,128)(2,1)S(1)}, bf16[8,2,16,896]{3,2,1,0:T(8,128)(2,1)S(1)}, u32[]{:S(2)}, u32[]{:S(2)}) collective-permute-start(bf16[8,2,16,896]{3,2,1,0:T(8,128)(2,1)S(1)} %collective-permute-done.4.refs_3_), channel_id=1, source_target_pairs={{0,32},{32,64},{64,96},{96,128},{128,160},{160,192},{192,224},{224... | collective-permute-start | bytes 1376264 | tf_op jit(solution)/shard_map/ppermute | solution.py:304
  146.4 7.3 %collective-permute-start.10 = (bf16[4,2,16,896]{3,2,1,0:T(8,128)(2,1)S(1)}, bf16[4,2,16,896]{3,2,1,0:T(8,128)(2,1)S(1)}, u32[]{:S(2)}, u32[]{:S(2)}) collective-permute-start(bf16[4,2,16,896]{3,2,1,0:T(8,128)(2,1)S(1)} %slice.27), channel_id=1, source_target_pairs={{0,224},{32,0},{64,32},{96,64},{128,96},{160,128},{192,160},{224,1... | collective-permute-start | bytes 688136 | tf_op jit(solution)/shard_map/ppermute | solution.py:309
  150.2 7.3 %collective-permute-start.8 = (bf16[4,2,16,896]{3,2,1,0:T(8,128)(2,1)S(1)}, bf16[4,2,16,896]{3,2,1,0:T(8,128)(2,1)S(1)}, u32[]{:S(2)}, u32[]{:S(2)}) collective-permute-start(bf16[4,2,16,896]{3,2,1,0:T(8,128)(2,1)S(1)} %slice.26), channel_id=1, source_target_pairs={{0,32},{32,64},{64,96},{96,128},{128,160},{160,192},{192,224},{224... | collective-permute-start | bytes 688136 | tf_op jit(solution)/shard_map/ppermute | solution.py:309
  150.3 14.4 %collective-permute-start.12 = (bf16[112,896]{1,0:T(8,128)(2,1)}, bf16[112,896]{1,0:T(8,128)(2,1)}, u32[]{:S(2)}, u32[]{:S(2)}) collective-permute-start(bf16[112,896]{1,0:T(8,128)(2,1)} %bitcast.58), channel_id=1, source_target_pairs={{0,16},{16,0},{1,17},{17,1},{2,18},{18,2},{3,19},{19,3},{4,20},{20... | collective-permute-start | bytes 602120 | tf_op jit(solution)/shard_map/ppermute | solution.py:282
  168.5 4.1 %collective-permute-start.13 = (bf16[8,8,16,896]{3,2,1,0:T(8,128)(2,1)S(1)}, bf16[8,8,16,896]{3,2,1,0:T(8,128)(2,1)S(1)}, u32[]{:S(2)}, u32[]{:S(2)}) collective-permute-start(bf16[8,8,16,896]{3,2,1,0:T(8,128)(2,1)S(1)} %bitcast_dynamic-update-slice_fusion), channel_id=1, source_target_pairs={{0,8},{8,0},{1,9},{9,1},{2,10},{10,2},{3,11},{11,3},{4,12},{12,4},... | collective-permute-start | bytes 5505032 | tf_op jit(solution)/shard_map/ppermute | solution.py:278
  187.4 54.8 %all-to-all-start.3 = ((bf16[8,224,896]{2,1,0:T(8,128)(2,1)}), bf16[8,224,896]{2,1,0:T(8,128)(2,1)}, u32[]{:S(2)}, u32[]{:S(2)}) async-start(bf16[8,224,896]{2,1,0:T(8,128)(2,1)} %get-tuple-element.43), calls=%async_computation.5 | async-start | bytes 6422528 | tf_op jit(solution)/shard_map/all_to_all | solution.py:388
  195.0 47.1 %copy-start.1 = (bf16[1,224,7168]{2,1,0:T(8,128)(2,1)S(1)}, bf16[1,224,7168]{2,1,0:T(8,128)(2,1)}, u32[]{:S(2)}) copy-start(bf16[1,224,7168]{2,1,0:T(8,128)(2,1)} %param.9) | copy-start | bytes 9633796
  214.1 28.1 %collective-permute-start.14 = (bf16[8,112,896]{2,1,0:T(8,128)(2,1)}, bf16[8,112,896]{2,1,0:T(8,128)(2,1)}, u32[]{:S(2)}, u32[]{:S(2)}) collective-permute-start(bf16[8,112,896]{2,1,0:T(8,128)(2,1)} %dynamic-slice_bitcast_fusion), channel_id=1, source_target_pairs={{0,8},{8,0},{1,9},{9,1},{2,10},{10,2},{3,11},{11,3},{4,12},{12,4},... | collective-permute-start | bytes 4816904 | tf_op jit(solution)/shard_map/ppermute | solution.py:278
  (10 other events, 42.8 us)
Sparse Core Ops, SparseCore 0:
  23.8 53.4 reduce-scatter.2
  79.8 42.5 reduce-scatter.4
  166.8 44.4 all-gather.1
